TPU v7x, 32 devices: a whole 2x2x4 slice. The times are simulated.
32 devices in a mesh: box: 32 (over z, y, x, core).
Axes of the slice: x: 2, y: 2, z: 4, core: 2. Of those that a mesh axis runs over, the one named last changes fastest.
Arguments:
- basis_vector: float32 [16, 131072], P(None, 'box'), may hold values from -600 to 600
- diagonal: float32 [131072], P('box'), may hold values from 0.25 to 2
- coords: int32 [2, 131072], P(None, 'box'), may hold values from 0 to 4095
- phase_scale: int32 [1], replicated, may hold values from 1 to 8190
- sketch_rows: int32 [131072], P('box'), may hold values from 0 to 2047
- sketch_signs: int32 [131072], P('box'), may hold values from 0 to 1
Outputs:
- new_basis: float32 [16, 131072], P(None, 'box')
- sketch: float32 [16, 2048], replicated
- arnoldi: float32 [2, 16], replicated
All inputs are finite; a program needn't handle non-finite values.
Results may differ from a plain program's by a relative error of at most 0.00019.
Values sent between devices are 32-bit elements; how exact they have to be, the bound alone decides.
A program may use at most 64 MiB of HBM per device.

v0:
```python
import functools
import math

import jax
import jax.numpy as jnp
import numpy as np
from jax import lax
from jax.experimental import pallas as pl
from jax.experimental.pallas import tpu as pltpu
from jax.sharding import PartitionSpec as P

WIDTH = 32
LEAF = 32
SKETCH = 2048
LANES = 128
HIGH = 8
LOW = SKETCH // HIGH
MODULUS = 8191
EPSILON = 1e-06
MESH = pl.DeviceIdType.MESH
F32 = jnp.float32
BF16 = jnp.bfloat16


def sine_series():
    node = np.cos((np.arange(400) + 0.5) * np.pi / 800)
    basis = np.stack([node ** (2 * i) for i in range(6)], 1)
    exact = np.sin(np.pi * node * 4096 / MODULUS) / node
    return np.linalg.lstsq(basis, exact, rcond=None)[0]


SERIES = sine_series()


def remainder(n):
    return n - jnp.floor(n * (1.0 / MODULUS) + 0.5) * float(MODULUS)


def half_sine(n, gain):
    t = remainder(n) * (1.0 / 4096)
    z = t * t
    total = z * float(SERIES[5] * gain) + float(SERIES[4] * gain)
    for c in SERIES[3::-1]:
        total = total * z + float(c * gain)
    return total * t


def scaled_cos(n, amplitude):
    s = half_sine(n, math.sqrt(2.0 * amplitude))
    return amplitude - s * s


def scaled_sin(n, amplitude):
    return scaled_cos(n - 0.25 * MODULUS, amplitude)


def fold(p):
    return (p & MODULUS) + lax.shift_right_logical(p, 13)


def kernel(devices, stages, total_points, scale_ref, v_ref, coords_ref, diag_ref, rows_ref, signs_ref,
           nb_ref, sketch_ref, arn_ref, raw, pts, leaf, mats, kk, cbuf, part, tbuf, work, onehot, skb, ski,
           a_send, a_recv, b_send, b_recv, sum_send, sum_recv, rs_send, rs_recv, ag_recv, own_chunk,
           a_ss, a_rs, b_ss, b_rs, s_ss, s_rs, r_ss, r_rs, g_ss, g_rs):
    me = lax.axis_index("box")
    columns = nb_ref.shape[0]
    halves = columns // 8
    barrier = pltpu.get_barrier_semaphore()

    @pl.loop(1, devices)
    def _(i):
        pl.semaphore_signal(barrier, inc=1, device_id=(lax.rem(me + i, devices),), device_id_type=MESH)

    lane = lax.broadcasted_iota(jnp.int32, (8, LANES), 1)
    sub = lax.broadcasted_iota(jnp.int32, (8, LANES), 0)
    scale = lax.rem(scale_ref[0], MODULUS)

    for r in range(LANES // 4):
        here = slice(LANES * r, LANES * (r + 1))
        for h in range(halves):
            raw[pl.ds(256 * h + r, 8, stride=32), :] = v_ref[8 * h:8 * h + 8, here]
        pair = coords_ref[:, here].astype(F32)
        raw[columns * 32 + r:columns * 32 + r + 1, :] = pair[0:1]
        raw[columns * 32 + 32 + r:columns * 32 + 33 + r, :] = pair[1:2]
    raw[(columns + 2) * 32:(columns + 3) * 32, :] = diag_ref[...]
    raw[(columns + 3) * 32:(columns + 4) * 32, :] = rows_ref[...].astype(F32)
    raw[(columns + 4) * 32:(columns + 5) * 32, :] = signs_ref[...].astype(F32)
    raw[(columns + 5) * 32:(columns + 8) * 32, :] = jnp.zeros((96, LANES), F32)
    for i in range((columns + 8) // 4):
        flipped = raw[LANES * i:LANES * (i + 1), :].T
        tbuf[0] = flipped
        for j in range(4):
            pts[4 * i + j] = jnp.concatenate(
                [tbuf[0, 32 * g:32 * g + 32, 32 * j:32 * j + 32] for g in range(4)], axis=1)

    def exact_phase(row):
        return fold(pts[columns + row].astype(jnp.int32) * scale).astype(F32)

    work[0] = exact_phase(0)
    work[1] = exact_phase(1)
    fx = (sub % 4 + 1).astype(F32)
    fy = (sub // 4 + 1).astype(F32)
    unit = 1.0 / math.sqrt(LEAF)

    @pl.loop(0, LEAF)
    def _(s):
        px = work[0, pl.ds(s, 1), :]
        py = work[1, pl.ds(s, 1), :]
        for tile in range(2):
            n = fx * px + (fy + 2.0 * tile) * py
            leaf[s, 8 * tile:8 * tile + 8] = scaled_cos(n, unit)
            leaf[s, 16 + 8 * tile:24 + 8 * tile] = scaled_sin(n, unit)

    def gather_half(h):
        def gather(s, acc):
            tiles = [leaf[s, 8 * t:8 * t + 8] for t in range(4)]
            out = []
            for q in range(8):
                row = pts[8 * h + q, pl.ds(s, 1), :]
                for t in range(4):
                    out.append(acc[4 * q + t] + tiles[t] * row)
            return tuple(out)

        acc = lax.fori_loop(0, LEAF, gather, tuple(jnp.zeros((8, LANES), F32) for _ in range(32)), unroll=2)
        for q in range(8):
            for t in range(4):
                cbuf[pl.ds((8 * h + q) * 32 + 8 * t, 8), :] = acc[4 * q + t]

    blocks = 8 * WIDTH // LANES

    def make_maps(low, bits):
        group = 2 ** bits
        places = LANES // group
        mine = lax.rem(me // 2 ** low, group)
        spot = mine * places + lane % places
        box = 4 * (spot % 32) + spot // 32
        member = me + (lane // places - mine) * 2 ** low
        ident = (member * LANES + box) * 37

        @pl.loop(low, low + bits)
        def _(k):
            x = (ident + 101 * k).astype(F32)
            rest = x - jnp.floor(x * (1.0 / (MODULUS - 1))) * float(MODULUS - 1)
            rest = jnp.where(rest < 0.0, rest + float(MODULUS - 1), rest)
            rest = jnp.where(rest >= float(MODULUS - 1), rest - float(MODULUS - 1), rest)
            key = rest.astype(jnp.int32) + 1
            unit_phase = fold(fold(key * scale)).astype(F32)
            wide = sub.astype(F32)
            for m in range(2):
                amplitude = (0.35 if m == 0 else 0.6) / math.sqrt(WIDTH)
                first, second, offset = (1.0, 2.0, 0.0) if m == 0 else (3.0, 1.0, 4096.0)
                mid = unit_phase * (wide + (8.0 + first))
                far = unit_phase * (wide + (16.0 + first))

                @pl.loop(0, WIDTH, unroll=2)
                def _(v):
                    times = v.astype(F32) + second
                    step = scaled_cos(unit_phase * (8.0 * times), 2.0)
                    one = scaled_cos(mid * times + offset, amplitude)
                    two = scaled_cos(far * times + offset, amplitude)
                    mats[2 * k + m, v, 8:16] = one
                    mats[2 * k + m, v, 16:24] = two
                    mats[2 * k + m, v, 0:8] = step * one - two
                    mats[2 * k + m, v, 24:32] = step * two - one

    def exchange(send, recv, ss, rs, low, bits, action):
        group = 2 ** bits
        mine = lax.rem(me // 2 ** low, group)

        @pl.loop(1, group)
        def _(i):
            other = lax.rem(mine + i, group)
            here = other if action is finish_recv else mine
            copy = pltpu.make_async_remote_copy(
                send.at[other], recv.at[here], ss.at[other], rs.at[here],
                device_id=(me + (other - mine) * 2 ** low,), device_id_type=MESH)
            action(copy)
        return mine

    def pack(send, group, h):
        places = LANES // group
        for j in range(blocks):
            at = LANES * (blocks * h + j)
            tbuf[j] = cbuf[at:at + LANES, :].T
        for d in range(group):
            for j in range(blocks):
                send[d, places * j:places * (j + 1), :] = tbuf[j, places * d:places * (d + 1), :]

    def unpack(recv, group, h):
        places = LANES // group
        for j in range(blocks):
            for d in range(group):
                tbuf[j, places * d:places * (d + 1), :] = recv[d, places * j:places * (j + 1), :]
        for j in range(blocks):
            at = LANES * (blocks * h + j)
            cbuf[at:at + LANES, :] = tbuf[j].T

    def sketch_of(values, target, make):
        target[...] = jnp.zeros_like(target)

        @pl.loop(0, LEAF // 4)
        def _(c):
            pieces = []
            for i in range(4):
                s = 4 * c + i
                row = pts[columns + 3, pl.ds(s, 1), :]
                high = jnp.floor(row * (1.0 / LOW))
                if make:
                    low = (row - high * LOW).astype(jnp.int32)
                    ids = lax.broadcasted_iota(jnp.int32, (LOW, LANES), 0)
                    onehot[c, :, LANES * i:LANES * (i + 1)] = jnp.where(ids == low, 1.0, 0.0).astype(BF16)
                sign = 2.0 * pts[columns + 4, pl.ds(s, 1), :] - 1.0
                v = values(s) * sign
                top = v.astype(BF16)
                rest = (v - top.astype(F32)).astype(BF16)
                wide = jnp.broadcast_to(high, (columns, LANES))
                masks = [jnp.where(wide == float(g), 1.0, 0.0).astype(BF16) for g in range(HIGH)]
                pieces.append(jnp.concatenate([top * g for g in masks] + [rest * g for g in masks], axis=0))
            left = jnp.concatenate(pieces, axis=1)
            target[...] += lax.dot_general(left, onehot[c], (((1,), (1,)), ((), ())), preferred_element_type=F32)

    nbt = kk

    def start(copy):
        copy.start()

    def finish_recv(copy):
        copy.wait_recv()

    def finish_send(copy):
        copy.wait_send()

    for index, (low, bits) in enumerate(stages):
        group = 2 ** bits
        places = LANES // group

        def outward(h, action):
            at = halves * index + h
            return exchange(a_send.at[at], a_recv.at[at], a_ss.at[at], a_rs.at[at], low, bits, action)

        def homeward(h, action):
            at = halves * index + h
            return exchange(b_send.at[at], b_recv.at[at], b_ss.at[at], b_rs.at[at], low, bits, action)

        for h in range(halves):
            at = halves * index + h
            if index == 0:
                gather_half(h)
            pack(a_send.at[at], group, h)
            if index == 0 and h == 0:
                pl.semaphore_wait(barrier, devices - 1)
            mine = outward(h, start)
            a_recv[at, mine] = a_send[at, mine]
        make_maps(low, bits)
        if index == 0:
            for q in range(columns):
                for s in range(LEAF):
                    nbt[s, q:q + 1, :] = pts[q, s:s + 1, :]
            sketch_of(lambda s: nbt[s], skb, True)
        for h in range(halves):
            at = halves * index + h
            outward(h, finish_recv)
            unpack(a_recv.at[at], group, h)
            half = slice(256 * h, 256 * (h + 1))
            for k in range(low, low + bits):
                span = places * 2 ** (k - low)
                full = cbuf[half, :]
                wide = lax.broadcasted_iota(jnp.int32, full.shape, 1)
                part[half, :] = jnp.where((wide // span) % 2 == 0,
                                          pltpu.roll(full, LANES - span, 1), pltpu.roll(full, span, 1))

                def mix(v, acc):
                    own = [mats[2 * k, v, 8 * t:8 * t + 8] for t in range(4)]
                    cross = [mats[2 * k + 1, v, 8 * t:8 * t + 8] for t in range(4)]
                    out = []
                    for q in range(8):
                        row = cbuf[pl.ds((8 * h + q) * 32 + v, 1), :]
                        other = part[pl.ds((8 * h + q) * 32 + v, 1), :]
                        for t in range(4):
                            out.append(acc[4 * q + t] + own[t] * row + cross[t] * other)
                    return tuple(out)

                init = tuple(0.85 * cbuf[pl.ds((8 * h + q) * 32 + 8 * t, 8), :] for q in range(8) for t in range(4))
                acc = lax.fori_loop(0, WIDTH, mix, init, unroll=2)
                for q in range(8):
                    for t in range(4):
                        cbuf[pl.ds((8 * h + q) * 32 + 8 * t, 8), :] = acc[4 * q + t]
            pack(b_send.at[at], group, h)
            mine = homeward(h, start)
            b_recv[at, mine] = b_send[at, mine]
        for h in range(halves):
            outward(h, finish_send)
        for h in range(halves):
            homeward(h, finish_recv)
            unpack(b_recv.at[halves * index + h], group, h)
        for h in range(halves):
            homeward(h, finish_send)

    for c in range(LEAF // 8):
        def spread_out(w, acc):
            coef = [cbuf[pl.ds(8 * h * 32 + w, 8, stride=32), :] for h in range(halves)]
            out = []
            for s in range(8):
                row = leaf[8 * c + s, pl.ds(w, 1), :]
                for h in range(halves):
                    out.append(acc[halves * s + h] + coef[h] * row)
            return tuple(out)

        init = tuple(
            jnp.broadcast_to(pts[columns + 2, 8 * c + s:8 * c + s + 1, :], (8, LANES)) * nbt[8 * c + s, 8 * h:8 * h + 8]
            for s in range(8) for h in range(halves))
        acc = lax.fori_loop(0, WIDTH, spread_out, init, unroll=2)
        for s in range(8):
            for h in range(halves):
                part[(8 * c + s) * columns + 8 * h:(8 * c + s) * columns + 8 * h + 8, :] = acc[halves * s + h]

    inner = jnp.zeros((columns, LANES), F32)
    square, energy = inner, inner
    for s in range(LEAF):
        v, image = nbt[s], part[s * columns:(s + 1) * columns, :]
        inner, square, energy = inner + v * image, square + v * v, energy + image * image
    lane_q = lax.broadcasted_iota(jnp.int32, (columns, LANES), 1)
    row_q = lax.broadcasted_iota(jnp.int32, (columns, LANES), 0)
    packed = jnp.zeros((columns, LANES), F32)
    for i, value in enumerate((inner, square, energy)):
        packed = jnp.where(lane_q == row_q + columns * i, jnp.sum(value, axis=1, keepdims=True), packed)
    sum_send[...] = jnp.sum(packed, axis=0, keepdims=True)

    def to_all(source, recv, ss, rs, action):
        @pl.loop(1, devices)
        def _(i):
            other = lax.rem(me + i, devices)
            here = other if action is finish_recv else me
            action(pltpu.make_async_remote_copy(
                source(other), recv.at[here], ss.at[other], rs.at[here],
                device_id=(other,), device_id_type=MESH))

    to_all(lambda d: sum_send, sum_recv, s_ss, s_rs, start)
    sum_recv[me] = sum_send[...]
    sketch_of(lambda s: part[pl.ds(pl.multiple_of(s * columns, columns), columns), :], ski, False)
    to_all(lambda d: sum_send, sum_recv, s_ss, s_rs, finish_recv)
    totals = jnp.sum(sum_recv[...], axis=0)

    def column(i):
        picked = jnp.where(lane_q == row_q + columns * i, jnp.broadcast_to(totals, (columns, LANES)), 0.0)
        return jnp.broadcast_to(jnp.sum(picked, axis=1, keepdims=True) * (1.0 / total_points), (columns, LANES))

    inner_mean, square_mean, energy_mean = column(0), column(1), column(2)
    projection = inner_mean / (square_mean + EPSILON)
    energy = energy_mean - 2.0 * projection * inner_mean + projection * projection * square_mean
    spread = jnp.sqrt(energy + EPSILON)
    inverse = 1.0 / spread
    for i, value in enumerate((projection, spread)):
        arn_ref[i:i + 1, :] = jnp.sum(jnp.where(lane_q == row_q, value, 0.0), axis=0, keepdims=True)[:, :columns]

    rows_each = rs_send.shape[1]
    factor = math.sqrt(SKETCH / total_points)
    lowest = HIGH * columns
    part_tiles = LOW // LANES
    for n in range(devices):
        flat = n * rows_each
        tile, row = flat // 8, flat % 8
        strip, side = tile // part_tiles, tile % part_tiles
        top = strip * 8 + row
        q0 = top % columns
        cols = slice(side * LANES, (side + 1) * LANES)
        img = ski[top:top + rows_each, cols] + ski[lowest + top:lowest + top + rows_each, cols]
        bas = skb[top:top + rows_each, cols] + skb[lowest + top:lowest + top + rows_each, cols]
        rs_send[n] = (img - projection[q0:q0 + rows_each] * bas) * (factor * inverse[q0:q0 + rows_each])
    to_all(lambda d: rs_send.at[d], rs_recv, r_ss, r_rs, start)
    rs_recv[me] = rs_send[me]

    for s in range(LEAF):
        pts_rows = (part[s * columns:(s + 1) * columns, :] - projection * nbt[s]) * inverse
        nbt[s] = pts_rows
    for q in range(columns):
        for s in range(LEAF):
            pts[q, s:s + 1, :] = nbt[s, q:q + 1, :]
    for i in range(columns // 4):
        for j in range(4):
            for g in range(4):
                tbuf[0, 32 * g:32 * g + 32, 32 * j:32 * j + 32] = pts[4 * i + j, :, 32 * g:32 * g + 32]
        raw[LANES * i:LANES * (i + 1), :] = tbuf[0].T
    for r in range(LANES // 4):
        for h in range(halves):
            nb_ref[8 * h:8 * h + 8, LANES * r:LANES * (r + 1)] = raw[pl.ds(256 * h + r, 8, stride=32), :]

    to_all(lambda d: rs_send.at[d], rs_recv, r_ss, r_rs, finish_recv)
    own_chunk[...] = jnp.sum(rs_recv[...], axis=0)
    to_all(lambda d: own_chunk, ag_recv, g_ss, g_rs, start)
    ag_recv[me] = own_chunk[...]
    to_all(lambda d: sum_send, sum_recv, s_ss, s_rs, finish_send)
    to_all(lambda d: rs_send.at[d], rs_recv, r_ss, r_rs, finish_send)
    to_all(lambda d: own_chunk, ag_recv, g_ss, g_rs, finish_recv)
    for n in range(devices):
        flat = n * rows_each
        tile, row = flat // 8, flat % 8
        strip, side = tile // part_tiles, tile % part_tiles
        top = strip * 8 + row
        q0, high = top % columns, top // columns
        begin = high * LOW + side * LANES
        sketch_ref[q0:q0 + rows_each, begin:begin + LANES] = ag_recv[n]
    to_all(lambda d: own_chunk, ag_recv, g_ss, g_rs, finish_send)


def body(basis_vector, diagonal, coords, phase_scale, sketch_rows, sketch_signs):
    columns, local_points = basis_vector.shape
    devices = lax.axis_size("box")
    sections = devices.bit_length() - 1
    count = -(-sections // 5)
    stages, low = [], 0
    for i in range(count):
        bits = (sections - low) // (count - i)
        stages.append((low, bits))
        low += bits
    group = 2 ** max(bits for _, bits in stages)
    group_rows = [columns * WIDTH // LANES * (LANES // 2 ** bits) for _, bits in stages]
    plane = (local_points // LANES, LANES)
    rows_each = HIGH * columns * LOW // LANES // devices
    vmem = pl.BlockSpec(memory_space=pltpu.VMEM)
    dma = pltpu.SemaphoreType.DMA
    count_rows = max(group_rows)
    halves = columns // 8
    new_basis, sketch, arn = pl.pallas_call(
        functools.partial(kernel, devices, stages, local_points * devices),
        out_shape=(
            jax.ShapeDtypeStruct((columns, local_points), F32),
            jax.ShapeDtypeStruct((columns, SKETCH), F32),
            jax.ShapeDtypeStruct((2, columns), F32)),
        in_specs=[pl.BlockSpec(memory_space=pltpu.SMEM), vmem, vmem, vmem, vmem, vmem],
        out_specs=(vmem, vmem, vmem),
        scratch_shapes=[
            pltpu.VMEM(((columns + 8) * LEAF, LANES), F32),
            pltpu.VMEM((columns + 8, LEAF, LANES), F32),
            pltpu.VMEM((LEAF, WIDTH, LANES), F32),
            pltpu.VMEM((2 * sections, WIDTH, WIDTH, LANES), F32),
            pltpu.VMEM((LEAF, columns, LANES), F32),
            pltpu.VMEM((columns * WIDTH, LANES), F32),
            pltpu.VMEM((columns * WIDTH, LANES), F32),
            pltpu.VMEM((columns * WIDTH // LANES, LANES, LANES), F32),
            pltpu.VMEM((2, LEAF, LANES), F32),
            pltpu.VMEM((LEAF // 4, LOW, 4 * LANES), BF16),
            pltpu.VMEM((2 * HIGH * columns, LOW), F32),
            pltpu.VMEM((2 * HIGH * columns, LOW), F32),
            pltpu.VMEM((count * halves, group, count_rows // halves, LANES), F32),
            pltpu.VMEM((count * halves, group, count_rows // halves, LANES), F32),
            pltpu.VMEM((count * halves, group, count_rows // halves, LANES), F32),
            pltpu.VMEM((count * halves, group, count_rows // halves, LANES), F32),
            pltpu.VMEM((1, LANES), F32),
            pltpu.VMEM((devices, 1, LANES), F32),
            pltpu.VMEM((devices, rows_each, LANES), F32),
            pltpu.VMEM((devices, rows_each, LANES), F32),
            pltpu.VMEM((devices, rows_each, LANES), F32),
            pltpu.VMEM((rows_each, LANES), F32),
            dma((count * halves, group)), dma((count * halves, group)), dma((count * halves, group)), dma((count * halves, group)),
            dma((devices,)), dma((devices,)), dma((devices,)), dma((devices,)), dma((devices,)), dma((devices,)),
        ],
        compiler_params=pltpu.CompilerParams(
            collective_id=0, has_side_effects=True, vmem_limit_bytes=60 * 2**20),
        name="gmres",
    )(phase_scale, basis_vector, coords, diagonal.reshape(plane), sketch_rows.reshape(plane),
      sketch_signs.reshape(plane))
    return new_basis, sketch, arn


def solution(mesh):
    placed = (P(None, "box"), P("box"), P(None, "box"), P(), P("box"), P("box"))
    return jax.shard_map(
        body, mesh=mesh, in_specs=placed, out_specs=(P(None, "box"), P(), P()), check_vma=False
    )
```

profile of v0, /device:TPU:0, one launch (start us, length us, event | category | flops | bytes accessed | tf_op | source)
XLA Modules:
  0.0 58.6 jit_solution(8470592065461624052)
XLA Ops:
  1.3 54.3 %gmres.1 = (f32[16,4096]{1,0:T(8,128)}, f32[16,2048]{1,0:T(8,128)}, f32[2,16]{1,0:T(2,128)}) custom-call(s32[1]{0:T(128)S(6)} %copy.12.scale_ref, f32[16,4096]{1,0:T(8,128)} %v_ref.1, s32[2,4096]{1,0:T(2,128)} %coords_ref.1, f32[32,128]{1,0:T(8,128)} %bitcast.3, s32[32,128]{1,0:T(8,128)} %bitcast.4, s32[32,128]{1,0:T(8,128)} %bitcast.5), custom_call_target="tpu_custom_call" | custom-call | tf_op jit(solution)/shard_map/gmres/pallas_call | solution.py:424
  55.6 0.0 copy-start
  55.6 1.7 %copy.13 = f32[16,4096]{1,0:T(8,128)} copy(f32[16,4096]{1,0:T(8,128)} %get-tuple-element.6) | data formatting | bytes 524288
  57.3 0.0 copy-done
  57.3 0.0 copy-start.1
  57.3 0.7 %copy.14 = f32[16,2048]{1,0:T(8,128)} copy(f32[16,2048]{1,0:T(8,128)S(1)} %copy-done) | data formatting | bytes 262144
  58.0 0.0 copy-done.1
  58.0 0.6 copy.15
Async XLA Ops:
  55.6 1.7 %copy-start = (f32[16,2048]{1,0:T(8,128)S(1)}, f32[16,2048]{1,0:T(8,128)}, u32[]{:S(2)}) copy-start(f32[16,2048]{1,0:T(8,128)} %get-tuple-element.7) | copy-start | bytes 393220
  57.3 0.7 %copy-start.1 = (f32[2,16]{1,0:T(2,128)S(1)}, f32[2,16]{1,0:T(2,128)}, u32[]{:S(2)}) copy-start(f32[2,16]{1,0:T(2,128)} %get-tuple-element.8) | copy-start | bytes 388
where the time goes:
time: 58.7 us; the launch traced here: 58.6 us
  Pallas kernels  54.3 us (93%)
  local copies, waits for them, and re-layouts  2.93 us (5%)
  between operations  1.3 us (2%)
    pallas_call x1, Pallas kernels, body(): pl.pallas_call(functools.partial(kernel, devices, stages, local_points *...  54.3 us
    unnamed x7, local copies, waits for them, and re-layouts  2.93 us

commit v1 on v0

--- a/solution.py
+++ b/solution.py
@@ -403,9 +403,332 @@
     to_all(lambda d: own_chunk, ag_recv, g_ss, g_rs, finish_send)
 
 
+def split(x):
+    top = x.astype(BF16)
+    return top, (x - top.astype(F32)).astype(BF16)
+
+
+def tile_kernel(devices, total_points, scale_ref, v_ref, coords_ref, diag_ref, rows_ref, signs_ref,
+                nb_ref, sketch_ref, arn_ref, small_send, small, vals, phases, steps, mats, leaf, state, coef,
+                image, back, skb, ski, proj, sum_send, sum_recv, rb_send, rb_recv, ri_send, ri_recv, ag_recv,
+                own_chunk, sems):
+    me = lax.axis_index("box")
+    columns = nb_ref.shape[0]
+    sections = devices.bit_length() - 1
+    per_tile = LANES // LEAF
+    half = LANES // 2
+    barrier = pltpu.get_barrier_semaphore()
+
+    @pl.loop(1, devices)
+    def _(i):
+        pl.semaphore_signal(barrier, inc=1, device_id=(lax.rem(me + i, devices),), device_id_type=MESH)
+
+    lane = lax.broadcasted_iota(jnp.int32, (8, LANES), 1)
+    sub = lax.broadcasted_iota(jnp.int32, (8, LANES), 0)
+    scale = lax.rem(scale_ref[0], MODULUS)
+
+    def to_all(source, recv, which):
+        @pl.loop(1, devices)
+        def _(i):
+            other = lax.rem(me + i, devices)
+            pltpu.make_async_remote_copy(
+                source(other), recv(me), sems.at[2 * which], sems.at[2 * which + 1],
+                device_id=(other,), device_id_type=MESH).start()
+
+    def finish(ref, which, side):
+        pltpu.make_async_copy(ref, ref, sems.at[2 * which + side]).wait()
+
+    def columns_at(ref, tile):
+        return ref.at[:, pl.ds(pl.multiple_of(tile * LANES, LANES), LANES)]
+
+    others = pl.ds(0, devices - 1)
+    side_rows = 5
+    side_part = pl.ds(0, side_rows)
+
+    rows_f, signs_f = rows_ref[...].astype(F32), signs_ref[...].astype(F32)
+    for e in range(devices):
+        here = slice(e * LANES, (e + 1) * LANES)
+        small_send[e, 0:2, :] = coords_ref[:, here].astype(F32)
+        small_send[e, 2:3, :] = diag_ref[e:e + 1, :]
+        small_send[e, 3:4, :] = rows_f[e:e + 1, :]
+        small_send[e, 4:5, :] = signs_f[e:e + 1, :]
+    pl.semaphore_wait(barrier, devices - 1)
+    to_all(lambda d: small_send.at[d, side_part], lambda d: small.at[d, side_part], 0)
+    to_all(lambda d: columns_at(v_ref, d), lambda d: vals.at[d], 1)
+    small[me] = small_send[me]
+    vals[me] = columns_at(v_ref, me)[...]
+
+    spot = lane // LEAF
+    inner_lane = (lane % LEAF).astype(F32)
+    for k in range(sections):
+        for g in range(devices // 8):
+            ident = ((8 * g + sub) * LANES + per_tile * me + spot) * 37
+            x = (ident + 101 * k).astype(F32)
+            rest = x - jnp.floor(x * (1.0 / (MODULUS - 1))) * float(MODULUS - 1)
+            rest = jnp.where(rest < 0.0, rest + float(MODULUS - 1), rest)
+            rest = jnp.where(rest >= float(MODULUS - 1), rest - float(MODULUS - 1), rest)
+            key = rest.astype(jnp.int32) + 1
+            unit_phase = fold(fold(key * scale)).astype(F32)
+            for m, second in enumerate((2.0, 1.0)):
+                phi = remainder(unit_phase * (inner_lane + second))
+                phases[2 * k + m, 8 * g:8 * g + 8, :] = phi
+                steps[2 * k + m, 8 * g:8 * g + 8, :] = scaled_cos(8.0 * phi, 2.0)
+
+    wide_sub = lax.broadcasted_iota(jnp.int32, (WIDTH, LANES), 0)
+    wide_lane = lax.broadcasted_iota(jnp.int32, (WIDTH, LANES), 1)
+    ident_part = jnp.where(wide_lane % WIDTH == wide_sub, 0.85, 0.0)
+    sub_f = sub.astype(F32)
+    for k in range(sections):
+        stride = 2 ** k
+
+        @pl.loop(0, devices // 2)
+        def _(pair):
+            first_tile = (pair // stride) * (2 * stride) + pair % stride
+            for bit in range(2):
+                d = first_tile + stride * bit
+                for m in range(2):
+                    amplitude = (0.35 if m == 0 else 0.6) / math.sqrt(WIDTH)
+                    first, offset = (1.0, 0.0) if m == 0 else (3.0, 4096.0)
+                    phi = phases[2 * k + m, pl.ds(d, 1), :]
+                    step = steps[2 * k + m, pl.ds(d, 1), :]
+                    one = scaled_cos(phi * (sub_f + (8.0 + first)) + offset, amplitude)
+                    two = scaled_cos(phi * (sub_f + (16.0 + first)) + offset, amplitude)
+                    full = jnp.concatenate([step * one - two, one, two, step * two - one], axis=0)
+                    if m == 0:
+                        full = full + ident_part
+                    top, low = split(full)
+                    begin = LANES * (bit if m == 0 else 1 - bit)
+                    mats[k, pair, 64 * bit:64 * bit + 32, begin:begin + LANES] = top
+                    mats[k, pair, 64 * bit + 32:64 * bit + 64, begin:begin + LANES] = low
+
+    lanes_q = lax.broadcasted_iota(jnp.int32, (columns, LANES), 1)
+    rows_q = lax.broadcasted_iota(jnp.int32, (columns, LANES), 0)
+
+    def sketch_of(values, row_of, sign_of, target):
+        target[...] = jnp.zeros_like(target)
+
+        @pl.loop(0, devices // 4)
+        def _(c):
+            pieces, hots = [], []
+            for i in range(4):
+                s = 4 * c + i
+                row = row_of(s)
+                high = jnp.floor(row * (1.0 / LOW))
+                low = (row - high * LOW).astype(jnp.int32)
+                ids = lax.broadcasted_iota(jnp.int32, (LOW, LANES), 0)
+                hots.append(jnp.where(ids == low, 1.0, 0.0).astype(BF16))
+                sign = 2.0 * sign_of(s) - 1.0
+                top, rest = split(values(s) * sign)
+                wide = jnp.broadcast_to(high, (columns, LANES))
+                masks = [jnp.where(wide == float(g), 1.0, 0.0).astype(BF16) for g in range(HIGH)]
+                pieces.append(jnp.concatenate([top * g for g in masks] + [rest * g for g in masks], axis=0))
+            left = jnp.concatenate(pieces, axis=1)
+            hot = jnp.concatenate(hots, axis=1)
+            target[...] += lax.dot_general(left, hot, (((1,), (1,)), ((), ())), preferred_element_type=F32)
+
+    rows_each = rb_send.shape[1]
+    factor = math.sqrt(SKETCH / total_points)
+    lowest = HIGH * columns
+    part_tiles = LOW // LANES
+
+    def pieces_of(sk, send):
+        for n in range(devices):
+            flat = n * rows_each
+            tile, row = flat // 8, flat % 8
+            strip, side = tile // part_tiles, tile % part_tiles
+            top = strip * 8 + row
+            cols = slice(side * LANES, (side + 1) * LANES)
+            send[n] = sk[top:top + rows_each, cols] + sk[lowest + top:lowest + top + rows_each, cols]
+
+    sketch_of(lambda s: columns_at(v_ref, s)[...], lambda s: rows_ref[pl.ds(s, 1), :].astype(F32),
+              lambda s: signs_ref[pl.ds(s, 1), :].astype(F32), skb)
+    pieces_of(skb, rb_send)
+    to_all(lambda d: rb_send.at[d], lambda d: rb_recv.at[d], 2)
+    rb_recv[me] = rb_send[me]
+
+    finish(small.at[others, side_part], 0, 1)
+    fx = (sub % 4 + 1).astype(F32)
+    fy = (sub // 4 + 1).astype(F32)
+    unit = 1.0 / math.sqrt(LEAF)
+
+    @pl.loop(0, devices)
+    def _(d):
+        pair = fold(small[d, 0:2, :].astype(jnp.int32) * scale).astype(F32)
+        px, py = pair[0:1], pair[1:2]
+        phases_of = [fx * px + (fy + 2.0 * t) * py for t in range(2)]
+        full = jnp.concatenate([scaled_cos(n, unit) for n in phases_of] + [scaled_sin(n, unit) for n in phases_of], axis=0)
+        top, low = split(full)
+        leaf[d, 0:32] = top
+        leaf[d, 32:64] = low
+
+    finish(vals.at[others], 1, 1)
+
+    point_masks = [jnp.where(lanes_q // LEAF == j, 1.0, 0.0).astype(BF16) for j in range(per_tile)]
+    column_masks = [jnp.where((wide_lane % half) // columns == j, 1.0, 0.0).astype(BF16) for j in range(per_tile)]
+    first_half = wide_lane < half
+
+    def combine(o):
+        s = o[0:32] + o[32:64]
+        return s + pltpu.roll(s, half, 1)
+
+    def expand(total):
+        top = total.astype(BF16).astype(F32)
+        y = jnp.where(first_half, top, total - top).astype(BF16)
+        return jnp.concatenate([y * m for m in column_masks], axis=0)
+
+    for d in range(devices):
+        top, rest = split(vals[d])
+        spread_v = jnp.concatenate([top * m for m in point_masks] + [rest * m for m in point_masks], axis=0)
+        o = lax.dot_general(leaf[d], spread_v, (((1,), (1,)), ((), ())), preferred_element_type=F32)
+        state[0, d] = expand(combine(o))
+
+    for k in range(sections):
+        stride = 2 ** k
+        now = k % 2
+        for pair in range(devices // 2):
+            d0 = (pair // stride) * (2 * stride) + pair % stride
+            d1 = d0 + stride
+            x = jnp.concatenate([state[now, d0], state[now, d1]], axis=0)
+            o = jnp.dot(mats[k, pair], x, preferred_element_type=F32)
+            for d, part in ((d0, o[0:64]), (d1, o[64:128])):
+                total = combine(part)
+                if k == sections - 1:
+                    coef[32 * d:32 * d + 32, :] = total
+                else:
+                    state[1 - now, d] = expand(total)
+
+    tile_lane = lax.broadcasted_iota(jnp.int32, (half, 2 * LANES), 1)
+    tile_masks = [jnp.where((tile_lane % LANES) // WIDTH == t, 1.0, 0.0).astype(BF16) for t in range(4)]
+    zero = jnp.zeros((columns, LANES), F32)
+    inner, square, energy = zero, zero, zero
+    for g in range(devices // 4):
+        flipped = coef[LANES * g:LANES * (g + 1), :].T
+        top, rest = split(flipped[0:half])
+        both = jnp.concatenate([top, rest], axis=1)
+        left = jnp.concatenate([both * m for m in tile_masks], axis=0)
+        tops = jnp.concatenate([leaf[4 * g + t, 0:32] for t in range(4)], axis=0)
+        lows = jnp.concatenate([leaf[4 * g + t, 32:64] for t in range(4)], axis=0)
+        right = jnp.concatenate([tops, lows], axis=1)
+        o = jnp.dot(left, jnp.concatenate([right, right], axis=0), preferred_element_type=F32)
+        o = o[:, 0:LANES] + o[:, LANES:2 * LANES]
+        for t in range(4):
+            d = 4 * g + t
+            v = vals[d]
+            img = jnp.broadcast_to(small[d, 2:3, :], (columns, LANES)) * v
+            for j in range(per_tile):
+                begin = half * t + columns * j
+                img = img + jnp.where(lanes_q // LEAF == j, o[begin:begin + columns], 0.0)
+            image[d] = img
+            inner, square, energy = inner + v * img, square + v * v, energy + img * img
+
+    packed = zero
+    for i, value in enumerate((inner, square, energy)):
+        packed = jnp.where(lanes_q == rows_q + columns * i, jnp.sum(value, axis=1, keepdims=True), packed)
+    sum_send[...] = jnp.sum(packed, axis=0, keepdims=True)
+    to_all(lambda d: sum_send, lambda d: sum_recv.at[d], 3)
+    sum_recv[me] = sum_send[...]
+
+    sketch_of(lambda d: image[d], lambda d: small[d, 3:4, :], lambda d: small[d, 4:5, :], ski)
+    pieces_of(ski, ri_send)
+    to_all(lambda d: ri_send.at[d], lambda d: ri_recv.at[d], 4)
+    ri_recv[me] = ri_send[me]
+    to_all(lambda d: image.at[d], lambda d: back.at[d], 5)
+    back[me] = image[me]
+
+    finish(small_send.at[others, side_part], 0, 0)
+    finish(vals.at[others], 1, 0)
+    finish(rb_send.at[others], 2, 0)
+    finish(rb_recv.at[others], 2, 1)
+    finish(sum_recv.at[others], 3, 0)
+    finish(sum_recv.at[others], 3, 1)
+    totals = jnp.sum(sum_recv[...], axis=0)
+
+    def column(i):
+        picked = jnp.where(lanes_q == rows_q + columns * i, jnp.broadcast_to(totals, (columns, LANES)), 0.0)
+        return jnp.broadcast_to(jnp.sum(picked, axis=1, keepdims=True) * (1.0 / total_points), (columns, LANES))
+
+    inner_mean, square_mean, energy_mean = column(0), column(1), column(2)
+    projection = inner_mean / (square_mean + EPSILON)
+    energy = energy_mean - 2.0 * projection * inner_mean + projection * projection * square_mean
+    spread = jnp.sqrt(energy + EPSILON)
+    inverse = 1.0 / spread
+    for i, value in enumerate((projection, spread)):
+        arn_ref[i:i + 1, :] = jnp.sum(jnp.where(lanes_q == rows_q, value, 0.0), axis=0, keepdims=True)[:, :columns]
+    proj[0] = projection
+    proj[1] = inverse * factor
+    mine = pl.ds(pl.multiple_of(lax.rem((me // part_tiles) * rows_each, columns), rows_each), rows_each)
+    base = jnp.sum(rb_recv[...], axis=0) * proj[0, mine, :]
+
+    finish(ri_recv.at[others], 4, 1)
+    own_chunk[...] = (jnp.sum(ri_recv[...], axis=0) - base) * proj[1, mine, :]
+    to_all(lambda d: own_chunk, lambda d: ag_recv.at[d], 6)
+    ag_recv[me] = own_chunk[...]
+    finish(back.at[others], 5, 1)
+    for e in range(devices):
+        here = slice(e * LANES, (e + 1) * LANES)
+        nb_ref[:, here] = (back[e] - projection * v_ref[:, here]) * inverse
+    finish(image.at[others], 5, 0)
+    finish(ri_send.at[others], 4, 0)
+    finish(ag_recv.at[others], 6, 0)
+    finish(ag_recv.at[others], 6, 1)
+    for n in range(devices):
+        flat = n * rows_each
+        tile, row = flat // 8, flat % 8
+        strip, side = tile // part_tiles, tile % part_tiles
+        top = strip * 8 + row
+        q0, high = top % columns, top // columns
+        begin = high * LOW + side * LANES
+        sketch_ref[q0:q0 + rows_each, begin:begin + LANES] = ag_recv[n]
+
+
+def together(devices, basis_vector, diagonal, coords, phase_scale, sketch_rows, sketch_signs):
+    columns, local_points = basis_vector.shape
+    sections = devices.bit_length() - 1
+    plane = (local_points // LANES, LANES)
+    rows_each = HIGH * columns * LOW // LANES // devices
+    vmem = pl.BlockSpec(memory_space=pltpu.VMEM)
+    tile = pltpu.VMEM((devices, columns, LANES), F32)
+    chunk = pltpu.VMEM((devices, rows_each, LANES), F32)
+    return pl.pallas_call(
+        functools.partial(tile_kernel, devices, local_points * devices),
+        out_shape=(
+            jax.ShapeDtypeStruct((columns, local_points), F32),
+            jax.ShapeDtypeStruct((columns, SKETCH), F32),
+            jax.ShapeDtypeStruct((2, columns), F32)),
+        in_specs=[pl.BlockSpec(memory_space=pltpu.SMEM), vmem, vmem, vmem, vmem, vmem],
+        out_specs=(vmem, vmem, vmem),
+        scratch_shapes=[
+            pltpu.VMEM((devices, 8, LANES), F32),
+            pltpu.VMEM((devices, 8, LANES), F32),
+            tile,
+            pltpu.VMEM((2 * sections, devices, LANES), F32),
+            pltpu.VMEM((2 * sections, devices, LANES), F32),
+            pltpu.VMEM((sections, devices // 2, 4 * WIDTH, 2 * LANES), BF16),
+            pltpu.VMEM((devices, 2 * WIDTH, LANES), BF16),
+            pltpu.VMEM((2, devices, LANES, LANES), BF16),
+            pltpu.VMEM((devices * WIDTH, LANES), F32),
+            tile, tile,
+            pltpu.VMEM((2 * HIGH * columns, LOW), F32),
+            pltpu.VMEM((2 * HIGH * columns, LOW), F32),
+            pltpu.VMEM((2, columns, LANES), F32),
+            pltpu.VMEM((1, LANES), F32),
+            pltpu.VMEM((devices, 1, LANES), F32),
+            chunk, chunk, chunk, chunk, chunk,
+            pltpu.VMEM((rows_each, LANES), F32),
+            pltpu.SemaphoreType.DMA((14,)),
+        ],
+        compiler_params=pltpu.CompilerParams(
+            collective_id=0, has_side_effects=True, vmem_limit_bytes=60 * 2**20),
+        name="gmres",
+    )(phase_scale, basis_vector, coords, diagonal.reshape(plane), sketch_rows.reshape(plane),
+      sketch_signs.reshape(plane))
+
+
 def body(basis_vector, diagonal, coords, phase_scale, sketch_rows, sketch_signs):
     columns, local_points = basis_vector.shape
     devices = lax.axis_size("box")
+    if devices * LANES == local_points:
+        return together(devices, basis_vector, diagonal, coords, phase_scale, sketch_rows, sketch_signs)
     sections = devices.bit_length() - 1
     count = -(-sections // 5)
     stages, low = [], 0

time: 58.7 us -> 41.5 us (0.71)
  Pallas kernels: 54.3 us -> 37.1 us
    pallas_call x1, Pallas kernels: 54.3 us -> 37.1 us  [together(): pl.pallas_call(functools.partial(tile_kernel, devices, local_points * dev...]
where the time goes in v1:
time: 41.5 us; the launch traced here: 41.4 us
  Pallas kernels  37.1 us (89%)
  local copies, waits for them, and re-layouts  2.93 us (7%)
  between operations  1.3 us (3%)
    pallas_call x1, Pallas kernels, together(): pl.pallas_call(functools.partial(tile_kernel, devices, local_points * dev...  37.1 us
    unnamed x7, local copies, waits for them, and re-layouts  2.93 us

profile of v1, /device:TPU:0, one launch (start us, length us, event | category | flops | bytes accessed | tf_op | source)
XLA Modules:
  0.0 41.4 jit_solution(3499557168715406249)
XLA Ops:
  1.3 37.1 %gmres.1 = (f32[16,4096]{1,0:T(8,128)}, f32[16,2048]{1,0:T(8,128)}, f32[2,16]{1,0:T(2,128)}) custom-call(s32[1]{0:T(128)S(6)} %copy.12.scale_ref, f32[16,4096]{1,0:T(8,128)} %v_ref.1, s32[2,4096]{1,0:T(2,128)} %coords_ref.1, f32[32,128]{1,0:T(8,128)} %bitcast.3, s32[32,128]{1,0:T(8,128)} %bitcast.4, s32[32,128]{1,0:T(8,128)} %bitcast.5), custom_call_target="tpu_custom_call" | custom-call | tf_op jit(solution)/shard_map/gmres/pallas_call | solution.py:692
  38.4 0.0 copy-start
  38.4 1.7 %copy.13 = f32[16,4096]{1,0:T(8,128)} copy(f32[16,4096]{1,0:T(8,128)} %get-tuple-element.6) | data formatting | bytes 524288
  40.1 0.0 copy-done
  40.1 0.0 copy-start.1
  40.1 0.7 %copy.14 = f32[16,2048]{1,0:T(8,128)} copy(f32[16,2048]{1,0:T(8,128)S(1)} %copy-done) | data formatting | bytes 262144
  40.8 0.0 copy-done.1
  40.8 0.6 %copy.15 = f32[2,16]{1,0:T(2,128)} copy(f32[2,16]{1,0:T(2,128)S(1)} %copy-done.1) | data formatting | bytes 256
Async XLA Ops:
  38.4 1.7 %copy-start = (f32[16,2048]{1,0:T(8,128)S(1)}, f32[16,2048]{1,0:T(8,128)}, u32[]{:S(2)}) copy-start(f32[16,2048]{1,0:T(8,128)} %get-tuple-element.7) | copy-start | bytes 393220
  40.1 0.7 %copy-start.1 = (f32[2,16]{1,0:T(2,128)S(1)}, f32[2,16]{1,0:T(2,128)}, u32[]{:S(2)}) copy-start(f32[2,16]{1,0:T(2,128)} %get-tuple-element.8) | copy-start | bytes 388

commit v2 on v1

--- a/solution.py
+++ b/solution.py
@@ -408,10 +408,11 @@
     return top, (x - top.astype(F32)).astype(BF16)
 
 
-def tile_kernel(devices, total_points, scale_ref, v_ref, coords_ref, diag_ref, rows_ref, signs_ref,
-                nb_ref, sketch_ref, arn_ref, small_send, small, vals, phases, steps, mats, leaf, state, coef,
-                image, back, skb, ski, proj, sum_send, sum_recv, rb_send, rb_recv, ri_send, ri_recv, ag_recv,
-                own_chunk, sems):
+def tile_kernel(devices, total_points, scale_ref, v_in, coords_in, diag_in, rows_in, signs_in,
+                nb_ref, sketch_ref, arn_ref, v_ref, coords_ref, diag_ref, rows_ref, signs_ref,
+                small_send, small, vals, phases, steps, mats, leaf, state, coef,
+                image, back, hot, left, masks, proj, sum_send, sum_recv, rb_send, rb_recv, ri_send, ri_recv,
+                ag_recv, own_chunk, sems, io_sems):
     me = lax.axis_index("box")
     columns = nb_ref.shape[0]
     sections = devices.bit_length() - 1
@@ -423,17 +424,29 @@
     def _(i):
         pl.semaphore_signal(barrier, inc=1, device_id=(lax.rem(me + i, devices),), device_id_type=MESH)
 
+    incoming = [pltpu.make_async_copy(a, b, io_sems.at[i]) for i, (a, b) in enumerate((
+        (v_in, v_ref), (coords_in, coords_ref), (diag_in, diag_ref), (rows_in, rows_ref), (signs_in, signs_ref)))]
+    for copy in incoming:
+        copy.start()
     lane = lax.broadcasted_iota(jnp.int32, (8, LANES), 1)
     sub = lax.broadcasted_iota(jnp.int32, (8, LANES), 0)
-    scale = lax.rem(scale_ref[0], MODULUS)
-
-    def to_all(source, recv, which):
-        @pl.loop(1, devices)
-        def _(i):
-            other = lax.rem(me + i, devices)
-            pltpu.make_async_remote_copy(
-                source(other), recv(me), sems.at[2 * which], sems.at[2 * which + 1],
-                device_id=(other,), device_id_type=MESH).start()
+    planes = 4
+    plane_size = devices // planes
+    plane, seat = me // plane_size, lax.rem(me, plane_size)
+
+    def to_all(source, recv, which, aways=range(planes - 1, -1, -1)):
+        for away in aways:
+            there = 0
+            for b in range(planes.bit_length() - 1):
+                bit = lax.rem(plane // 2 ** b, 2)
+                there = there + 2 ** b * ((1 - bit) if (away >> b) & 1 else bit)
+
+            @pl.loop(0 if away else 1, plane_size)
+            def _(i):
+                other = plane_size * there + lax.rem(seat + i, plane_size)
+                pltpu.make_async_remote_copy(
+                    source(other), recv(me), sems.at[2 * which], sems.at[2 * which + 1],
+                    device_id=(other,), device_id_type=MESH).start()
 
     def finish(ref, which, side):
         pltpu.make_async_copy(ref, ref, sems.at[2 * which + side]).wait()
@@ -445,6 +458,9 @@
     side_rows = 5
     side_part = pl.ds(0, side_rows)
 
+    for copy in incoming:
+        copy.wait()
+    scale = lax.rem(scale_ref[0], MODULUS)
     rows_f, signs_f = rows_ref[...].astype(F32), signs_ref[...].astype(F32)
     for e in range(devices):
         here = slice(e * LANES, (e + 1) * LANES)
@@ -504,31 +520,35 @@
     lanes_q = lax.broadcasted_iota(jnp.int32, (columns, LANES), 1)
     rows_q = lax.broadcasted_iota(jnp.int32, (columns, LANES), 0)
 
-    def sketch_of(values, row_of, sign_of, target):
-        target[...] = jnp.zeros_like(target)
-
-        @pl.loop(0, devices // 4)
-        def _(c):
-            pieces, hots = [], []
-            for i in range(4):
-                s = 4 * c + i
-                row = row_of(s)
-                high = jnp.floor(row * (1.0 / LOW))
-                low = (row - high * LOW).astype(jnp.int32)
-                ids = lax.broadcasted_iota(jnp.int32, (LOW, LANES), 0)
-                hots.append(jnp.where(ids == low, 1.0, 0.0).astype(BF16))
-                sign = 2.0 * sign_of(s) - 1.0
-                top, rest = split(values(s) * sign)
-                wide = jnp.broadcast_to(high, (columns, LANES))
-                masks = [jnp.where(wide == float(g), 1.0, 0.0).astype(BF16) for g in range(HIGH)]
-                pieces.append(jnp.concatenate([top * g for g in masks] + [rest * g for g in masks], axis=0))
-            left = jnp.concatenate(pieces, axis=1)
-            hot = jnp.concatenate(hots, axis=1)
-            target[...] += lax.dot_general(left, hot, (((1,), (1,)), ((), ())), preferred_element_type=F32)
+    def place(tile):
+        return pl.ds(pl.multiple_of(tile * LANES, LANES), LANES)
+
+    def make_hot(row_of, sign_of):
+        @pl.loop(0, devices)
+        def _(d):
+            row = row_of(d)
+            high = jnp.floor(row * (1.0 / LOW))
+            low = (row - high * LOW).astype(jnp.int32)
+            ids = lax.broadcasted_iota(jnp.int32, (LOW, LANES), 0)
+            hot[:, place(d)] = jnp.where(ids == low, 1.0, 0.0).astype(BF16)
+            sign = jnp.broadcast_to(2.0 * sign_of(d) - 1.0, (columns, LANES))
+            wide = jnp.broadcast_to(high, (columns, LANES))
+            for g in range(HIGH):
+                masks[d, columns * g:columns * (g + 1), :] = jnp.where(wide == float(g), sign, 0.0).astype(BF16)
+
+    def place_values(d, at, value):
+        top, rest = split(value)
+        for g in range(HIGH):
+            mask = masks[d, columns * g:columns * (g + 1), :]
+            left[columns * g:columns * (g + 1), at] = top * mask
+            left[columns * (HIGH + g):columns * (HIGH + g + 1), at] = rest * mask
+
+    def sketch_product():
+        o = lax.dot_general(left[...], hot[...], (((1,), (1,)), ((), ())), preferred_element_type=F32)
+        return o[:HIGH * columns] + o[HIGH * columns:]
 
     rows_each = rb_send.shape[1]
     factor = math.sqrt(SKETCH / total_points)
-    lowest = HIGH * columns
     part_tiles = LOW // LANES
 
     def pieces_of(sk, send):
@@ -538,13 +558,16 @@
             strip, side = tile // part_tiles, tile % part_tiles
             top = strip * 8 + row
             cols = slice(side * LANES, (side + 1) * LANES)
-            send[n] = sk[top:top + rows_each, cols] + sk[lowest + top:lowest + top + rows_each, cols]
-
-    sketch_of(lambda s: columns_at(v_ref, s)[...], lambda s: rows_ref[pl.ds(s, 1), :].astype(F32),
-              lambda s: signs_ref[pl.ds(s, 1), :].astype(F32), skb)
-    pieces_of(skb, rb_send)
-    to_all(lambda d: rb_send.at[d], lambda d: rb_recv.at[d], 2)
-    rb_recv[me] = rb_send[me]
+            send[n] = sk[top:top + rows_each, cols]
+
+    make_hot(lambda d: rows_ref[pl.ds(d, 1), :].astype(F32), lambda d: signs_ref[pl.ds(d, 1), :].astype(F32))
+
+    @pl.loop(0, devices)
+    def _(d):
+        place_values(d, place(d), v_ref[:, place(d)])
+
+    basis_sketch = sketch_product()
+    pieces_of(basis_sketch, rb_send)
 
     finish(small.at[others, side_part], 0, 1)
     fx = (sub % 4 + 1).astype(F32)
@@ -561,7 +584,10 @@
         leaf[d, 0:32] = top
         leaf[d, 32:64] = low
 
+    make_hot(lambda d: small[d, 3:4, :], lambda d: small[d, 4:5, :])
     finish(vals.at[others], 1, 1)
+    to_all(lambda d: rb_send.at[d], lambda d: rb_recv.at[d], 2)
+    rb_recv[me] = rb_send[me]
 
     point_masks = [jnp.where(lanes_q // LEAF == j, 1.0, 0.0).astype(BF16) for j in range(per_tile)]
     column_masks = [jnp.where((wide_lane % half) // columns == j, 1.0, 0.0).astype(BF16) for j in range(per_tile)]
@@ -605,11 +631,11 @@
         flipped = coef[LANES * g:LANES * (g + 1), :].T
         top, rest = split(flipped[0:half])
         both = jnp.concatenate([top, rest], axis=1)
-        left = jnp.concatenate([both * m for m in tile_masks], axis=0)
+        lhs = jnp.concatenate([both * m for m in tile_masks], axis=0)
         tops = jnp.concatenate([leaf[4 * g + t, 0:32] for t in range(4)], axis=0)
         lows = jnp.concatenate([leaf[4 * g + t, 32:64] for t in range(4)], axis=0)
         right = jnp.concatenate([tops, lows], axis=1)
-        o = jnp.dot(left, jnp.concatenate([right, right], axis=0), preferred_element_type=F32)
+        o = jnp.dot(lhs, jnp.concatenate([right, right], axis=0), preferred_element_type=F32)
         o = o[:, 0:LANES] + o[:, LANES:2 * LANES]
         for t in range(4):
             d = 4 * g + t
@@ -619,6 +645,7 @@
                 begin = half * t + columns * j
                 img = img + jnp.where(lanes_q // LEAF == j, o[begin:begin + columns], 0.0)
             image[d] = img
+            place_values(d, slice(LANES * d, LANES * (d + 1)), img)
             inner, square, energy = inner + v * img, square + v * v, energy + img * img
 
     packed = zero
@@ -628,11 +655,12 @@
     to_all(lambda d: sum_send, lambda d: sum_recv.at[d], 3)
     sum_recv[me] = sum_send[...]
 
-    sketch_of(lambda d: image[d], lambda d: small[d, 3:4, :], lambda d: small[d, 4:5, :], ski)
-    pieces_of(ski, ri_send)
+    to_all(lambda d: image.at[d], lambda d: back.at[d], 5, (3,))
+    image_sketch = sketch_product()
+    pieces_of(image_sketch, ri_send)
     to_all(lambda d: ri_send.at[d], lambda d: ri_recv.at[d], 4)
     ri_recv[me] = ri_send[me]
-    to_all(lambda d: image.at[d], lambda d: back.at[d], 5)
+    to_all(lambda d: image.at[d], lambda d: back.at[d], 5, (2, 1, 0))
     back[me] = image[me]
 
     finish(small_send.at[others, side_part], 0, 0)
@@ -686,6 +714,7 @@
     sections = devices.bit_length() - 1
     plane = (local_points // LANES, LANES)
     rows_each = HIGH * columns * LOW // LANES // devices
+    far = pl.BlockSpec(memory_space=pltpu.HBM)
     vmem = pl.BlockSpec(memory_space=pltpu.VMEM)
     tile = pltpu.VMEM((devices, columns, LANES), F32)
     chunk = pltpu.VMEM((devices, rows_each, LANES), F32)
@@ -695,9 +724,14 @@
             jax.ShapeDtypeStruct((columns, local_points), F32),
             jax.ShapeDtypeStruct((columns, SKETCH), F32),
             jax.ShapeDtypeStruct((2, columns), F32)),
-        in_specs=[pl.BlockSpec(memory_space=pltpu.SMEM), vmem, vmem, vmem, vmem, vmem],
-        out_specs=(vmem, vmem, vmem),
+        in_specs=[pl.BlockSpec(memory_space=pltpu.SMEM)] + [far] * 5,
+        out_specs=(vmem,) * 3,
         scratch_shapes=[
+            pltpu.VMEM(basis_vector.shape, F32),
+            pltpu.VMEM(coords.shape, jnp.int32),
+            pltpu.VMEM(plane, F32),
+            pltpu.VMEM(plane, jnp.int32),
+            pltpu.VMEM(plane, jnp.int32),
             pltpu.VMEM((devices, 8, LANES), F32),
             pltpu.VMEM((devices, 8, LANES), F32),
             tile,
@@ -708,20 +742,23 @@
             pltpu.VMEM((2, devices, LANES, LANES), BF16),
             pltpu.VMEM((devices * WIDTH, LANES), F32),
             tile, tile,
-            pltpu.VMEM((2 * HIGH * columns, LOW), F32),
-            pltpu.VMEM((2 * HIGH * columns, LOW), F32),
+            pltpu.VMEM((LOW, local_points), BF16),
+            pltpu.VMEM((2 * HIGH * columns, local_points), BF16),
+            pltpu.VMEM((devices, HIGH * columns, LANES), BF16),
             pltpu.VMEM((2, columns, LANES), F32),
             pltpu.VMEM((1, LANES), F32),
             pltpu.VMEM((devices, 1, LANES), F32),
             chunk, chunk, chunk, chunk, chunk,
             pltpu.VMEM((rows_each, LANES), F32),
             pltpu.SemaphoreType.DMA((14,)),
+            pltpu.SemaphoreType.DMA((5,)),
         ],
         compiler_params=pltpu.CompilerParams(
-            collective_id=0, has_side_effects=True, vmem_limit_bytes=60 * 2**20),
+            collective_id=0, has_side_effects=True, vmem_limit_bytes=24 * 2**20),
         name="gmres",
-    )(phase_scale, basis_vector, coords, diagonal.reshape(plane), sketch_rows.reshape(plane),
-      sketch_signs.reshape(plane))
+    )(phase_scale, *(pltpu.with_memory_space_constraint(x, pltpu.HBM) for x in (
+        basis_vector, coords, diagonal.reshape(plane), sketch_rows.reshape(plane),
+        sketch_signs.reshape(plane))))
 
 
 def body(basis_vector, diagonal, coords, phase_scale, sketch_rows, sketch_signs):

time: 41.5 us -> 39.5 us (0.952)
  local copies, waits for them, and re-layouts: 2.93 us -> 1.92 us
  Pallas kernels: 37.1 us -> 36.1 us
    pallas_call x1, Pallas kernels: 37.1 us -> 36.1 us  [together(): pl.pallas_call(functools.partial(tile_kernel, devices, local_points * dev...]
    unnamed x7 -> x3, local copies, waits for them, and re-layouts: 2.93 us -> 1.92 us
where the time goes in v2:
time: 39.5 us; the launch traced here: 39.3 us
  Pallas kernels  36.1 us (91%)
  local copies, waits for them, and re-layouts  1.92 us (5%)
  between operations  1.29 us (3%)
    pallas_call x1, Pallas kernels, together(): pl.pallas_call(functools.partial(tile_kernel, devices, local_points * dev...  36.1 us
    unnamed x3, local copies, waits for them, and re-layouts  1.92 us

profile of v2, /device:TPU:0, one launch (start us, length us, event | category | flops | bytes accessed | tf_op | source)
XLA Modules:
  0.0 39.3 jit_solution(13928733868737880968)
XLA Ops:
  1.3 36.1 %gmres.1 = (f32[16,4096]{1,0:T(8,128)S(1)}, f32[16,2048]{1,0:T(8,128)S(1)}, f32[2,16]{1,0:T(2,128)S(1)}) custom-call(s32[1]{0:T(128)S(6)} %copy.12.scale_ref, f32[16,4096]{1,0:T(8,128)} %v_in.1, s32[2,4096]{1,0:T(2,128)} %coords_in.1, f32[32,128]{1,0:T(8,128)} %bitcast.3, s32[32,128]{1,0:T(8,128)} %bitcast.4, s32[32,128]{1,0:T(8,128)} %bitcast.5), custom_call_target="tpu_custom_call" | custom-call | tf_op jit(solution)/shard_map/gmres/pallas_call | solution.py:721
  37.4 0.7 %copy.13 = f32[16,4096]{1,0:T(8,128)} copy(f32[16,4096]{1,0:T(8,128)S(1)} %get-tuple-element.6) | data formatting | bytes 524288
  38.1 0.7 %copy.14 = f32[16,2048]{1,0:T(8,128)} copy(f32[16,2048]{1,0:T(8,128)S(1)} %get-tuple-element.7) | data formatting | bytes 262144
  38.8 0.6 %copy.15 = f32[2,16]{1,0:T(2,128)} copy(f32[2,16]{1,0:T(2,128)S(1)} %get-tuple-element.8) | data formatting | bytes 256

commit v3 on v2

--- a/solution.py
+++ b/solution.py
@@ -411,8 +411,9 @@
 def tile_kernel(devices, total_points, scale_ref, v_in, coords_in, diag_in, rows_in, signs_in,
                 nb_ref, sketch_ref, arn_ref, v_ref, coords_ref, diag_ref, rows_ref, signs_ref,
                 small_send, small, vals, phases, steps, mats, leaf, state, coef,
-                image, back, hot, left, masks, proj, sum_send, sum_recv, rb_send, rb_recv, ri_send, ri_recv,
-                ag_recv, own_chunk, sems, io_sems):
+                image, back, hot, left, masks, sum_send, sum_recv, sum_total, sum_joined, rb_send,
+                rb_recv, rb_total, rb_joined, ri_send, ri_recv, ri_total, ri_joined, ag_recv, own_chunk, sems,
+                io_sems):
     me = lax.axis_index("box")
     columns = nb_ref.shape[0]
     sections = devices.bit_length() - 1
@@ -433,34 +434,52 @@
     planes = 4
     plane_size = devices // planes
     plane, seat = me // plane_size, lax.rem(me, plane_size)
-
-    def to_all(source, recv, which, aways=range(planes - 1, -1, -1)):
+    halves = devices // 2
+    side = plane // 2
+
+    def facing(away):
+        there = 0
+        for b in range(planes.bit_length() - 1):
+            bit = lax.rem(plane // 2 ** b, 2)
+            there = there + 2 ** b * ((1 - bit) if (away >> b) & 1 else bit)
+        return there
+
+    def send(source, target, which, other):
+        pltpu.make_async_remote_copy(
+            source, target, sems.at[2 * which], sems.at[2 * which + 1],
+            device_id=(other,), device_id_type=MESH).start()
+
+    def to_all(source, target, which, aways):
         for away in aways:
-            there = 0
-            for b in range(planes.bit_length() - 1):
-                bit = lax.rem(plane // 2 ** b, 2)
-                there = there + 2 ** b * ((1 - bit) if (away >> b) & 1 else bit)
+            there = facing(away)
 
             @pl.loop(0 if away else 1, plane_size)
             def _(i):
                 other = plane_size * there + lax.rem(seat + i, plane_size)
-                pltpu.make_async_remote_copy(
-                    source(other), recv(me), sems.at[2 * which], sems.at[2 * which + 1],
-                    device_id=(other,), device_id_type=MESH).start()
-
-    def finish(ref, which, side):
-        pltpu.make_async_copy(ref, ref, sems.at[2 * which + side]).wait()
+                send(source(other), target, which, other)
+
+    def to_plane(source, target, which):
+        @pl.loop(1, plane_size)
+        def _(i):
+            other = lax.rem(seat + i, plane_size)
+            send(source(other), target, which, plane_size * plane + other)
+
+    def to_planes(source, target, which):
+        for away in range(planes - 1, 0, -1):
+            send(source, target, which, plane_size * facing(away) + seat)
+
+    def finish(ref, which, end):
+        pltpu.make_async_copy(ref, ref, sems.at[2 * which + end]).wait()
 
     def columns_at(ref, tile):
         return ref.at[:, pl.ds(pl.multiple_of(tile * LANES, LANES), LANES)]
 
-    others = pl.ds(0, devices - 1)
+    others, mates, peers = pl.ds(0, devices - 1), pl.ds(0, plane_size - 1), pl.ds(0, planes - 1)
     side_rows = 5
     side_part = pl.ds(0, side_rows)
 
     for copy in incoming:
         copy.wait()
-    scale = lax.rem(scale_ref[0], MODULUS)
     rows_f, signs_f = rows_ref[...].astype(F32), signs_ref[...].astype(F32)
     for e in range(devices):
         here = slice(e * LANES, (e + 1) * LANES)
@@ -468,12 +487,7 @@
         small_send[e, 2:3, :] = diag_ref[e:e + 1, :]
         small_send[e, 3:4, :] = rows_f[e:e + 1, :]
         small_send[e, 4:5, :] = signs_f[e:e + 1, :]
-    pl.semaphore_wait(barrier, devices - 1)
-    to_all(lambda d: small_send.at[d, side_part], lambda d: small.at[d, side_part], 0)
-    to_all(lambda d: columns_at(v_ref, d), lambda d: vals.at[d], 1)
-    small[me] = small_send[me]
-    vals[me] = columns_at(v_ref, me)[...]
-
+    scale = lax.rem(scale_ref[0], MODULUS)
     spot = lane // LEAF
     inner_lane = (lane % LEAF).astype(F32)
     for k in range(sections):
@@ -494,10 +508,14 @@
     wide_lane = lax.broadcasted_iota(jnp.int32, (WIDTH, LANES), 1)
     ident_part = jnp.where(wide_lane % WIDTH == wide_sub, 0.85, 0.0)
     sub_f = sub.astype(F32)
-    for k in range(sections):
+    def make_maps(begins, ends):
+        for k in range(sections):
+            maps_of(k, begins[k], ends[k])
+
+    def maps_of(k, begin_pair, end_pair):
         stride = 2 ** k
 
-        @pl.loop(0, devices // 2)
+        @pl.loop(begin_pair, end_pair)
         def _(pair):
             first_tile = (pair // stride) * (2 * stride) + pair % stride
             for bit in range(2):
@@ -517,15 +535,29 @@
                     mats[k, pair, 64 * bit:64 * bit + 32, begin:begin + LANES] = top
                     mats[k, pair, 64 * bit + 32:64 * bit + 64, begin:begin + LANES] = low
 
+    hops = lax.rem(me // 2, 2) + lax.rem(me // 4, 2) + plane
+    budget = 18 * (5 - hops) - 8
+    early = [jnp.clip(budget - k * (devices // 2), 0, devices // 2) for k in range(sections)]
+    make_maps([0] * sections, early)
+    pl.semaphore_wait(barrier, devices - 1)
+    for which, aways in ((0, (3, 2)), (7, (1, 0))):
+        to_all(lambda d: small_send.at[d, side_part], small.at[me, side_part], which, aways)
+    for which, aways in ((1, (3, 2)), (8, (1, 0))):
+        to_all(lambda d: columns_at(v_ref, d), vals.at[me], which, aways)
+    small[me] = small_send[me]
+    vals[me] = columns_at(v_ref, me)[...]
+
+    make_maps(early, [devices // 2] * sections)
     lanes_q = lax.broadcasted_iota(jnp.int32, (columns, LANES), 1)
     rows_q = lax.broadcasted_iota(jnp.int32, (columns, LANES), 0)
 
     def place(tile):
         return pl.ds(pl.multiple_of(tile * LANES, LANES), LANES)
 
-    def make_hot(row_of, sign_of):
-        @pl.loop(0, devices)
-        def _(d):
+    def make_hot(row_of, sign_of, begin, count):
+        @pl.loop(0, count)
+        def _(i):
+            d = begin + i
             row = row_of(d)
             high = jnp.floor(row * (1.0 / LOW))
             low = (row - high * LOW).astype(jnp.int32)
@@ -547,48 +579,32 @@
         o = lax.dot_general(left[...], hot[...], (((1,), (1,)), ((), ())), preferred_element_type=F32)
         return o[:HIGH * columns] + o[HIGH * columns:]
 
-    rows_each = rb_send.shape[1]
     factor = math.sqrt(SKETCH / total_points)
-    part_tiles = LOW // LANES
-
-    def pieces_of(sk, send):
-        for n in range(devices):
-            flat = n * rows_each
-            tile, row = flat // 8, flat % 8
-            strip, side = tile // part_tiles, tile % part_tiles
-            top = strip * 8 + row
-            cols = slice(side * LANES, (side + 1) * LANES)
-            send[n] = sk[top:top + rows_each, cols]
-
-    make_hot(lambda d: rows_ref[pl.ds(d, 1), :].astype(F32), lambda d: signs_ref[pl.ds(d, 1), :].astype(F32))
+
+    def start_reduce(sk, pieces, landed, which):
+        for n in range(plane_size):
+            pieces[n] = sk[columns * n:columns * (n + 1), :]
+        to_plane(lambda n: pieces.at[n], landed.at[seat], which)
+        landed[seat] = pieces[seat]
+
+    def next_reduce(landed, total, joined, which, first):
+        finish(landed.at[pl.ds(0, plane_size - 1)], first, 1)
+        total[...] = jnp.sum(landed[...], axis=0)
+        to_planes(total, joined.at[plane], which)
+        joined[plane] = total[...]
+
+    make_hot(lambda d: rows_ref[pl.ds(d, 1), :].astype(F32), lambda d: signs_ref[pl.ds(d, 1), :].astype(F32), 0, devices)
 
     @pl.loop(0, devices)
     def _(d):
         place_values(d, place(d), v_ref[:, place(d)])
 
     basis_sketch = sketch_product()
-    pieces_of(basis_sketch, rb_send)
-
-    finish(small.at[others, side_part], 0, 1)
+    start_reduce(basis_sketch, rb_send, rb_recv, 2)
+
     fx = (sub % 4 + 1).astype(F32)
     fy = (sub // 4 + 1).astype(F32)
     unit = 1.0 / math.sqrt(LEAF)
-
-    @pl.loop(0, devices)
-    def _(d):
-        pair = fold(small[d, 0:2, :].astype(jnp.int32) * scale).astype(F32)
-        px, py = pair[0:1], pair[1:2]
-        phases_of = [fx * px + (fy + 2.0 * t) * py for t in range(2)]
-        full = jnp.concatenate([scaled_cos(n, unit) for n in phases_of] + [scaled_sin(n, unit) for n in phases_of], axis=0)
-        top, low = split(full)
-        leaf[d, 0:32] = top
-        leaf[d, 32:64] = low
-
-    make_hot(lambda d: small[d, 3:4, :], lambda d: small[d, 4:5, :])
-    finish(vals.at[others], 1, 1)
-    to_all(lambda d: rb_send.at[d], lambda d: rb_recv.at[d], 2)
-    rb_recv[me] = rb_send[me]
-
     point_masks = [jnp.where(lanes_q // LEAF == j, 1.0, 0.0).astype(BF16) for j in range(per_tile)]
     column_masks = [jnp.where((wide_lane % half) // columns == j, 1.0, 0.0).astype(BF16) for j in range(per_tile)]
     first_half = wide_lane < half
@@ -602,20 +618,34 @@
         y = jnp.where(first_half, top, total - top).astype(BF16)
         return jnp.concatenate([y * m for m in column_masks], axis=0)
 
-    for d in range(devices):
-        top, rest = split(vals[d])
-        spread_v = jnp.concatenate([top * m for m in point_masks] + [rest * m for m in point_masks], axis=0)
-        o = lax.dot_general(leaf[d], spread_v, (((1,), (1,)), ((), ())), preferred_element_type=F32)
-        state[0, d] = expand(combine(o))
-
-    for k in range(sections):
+    def leaves(begin):
+        @pl.loop(0, halves)
+        def _(i):
+            d = begin + i
+            pair = fold(small[d, 0:2, :].astype(jnp.int32) * scale).astype(F32)
+            px, py = pair[0:1], pair[1:2]
+            phases_of = [fx * px + (fy + 2.0 * t) * py for t in range(2)]
+            full = jnp.concatenate([scaled_cos(n, unit) for n in phases_of] + [scaled_sin(n, unit) for n in phases_of], axis=0)
+            top, low = split(full)
+            leaf[d, 0:32] = top
+            leaf[d, 32:64] = low
+
+    def gather(begin):
+        for i in range(halves):
+            d = begin + i
+            top, rest = split(vals[d])
+            spread_v = jnp.concatenate([top * m for m in point_masks] + [rest * m for m in point_masks], axis=0)
+            o = lax.dot_general(leaf[d], spread_v, (((1,), (1,)), ((), ())), preferred_element_type=F32)
+            state[0, d] = expand(combine(o))
+
+    def section(k, begin, count):
         stride = 2 ** k
         now = k % 2
-        for pair in range(devices // 2):
-            d0 = (pair // stride) * (2 * stride) + pair % stride
+        for i in range(count // 2):
+            d0 = begin + (i // stride) * (2 * stride) + i % stride
             d1 = d0 + stride
             x = jnp.concatenate([state[now, d0], state[now, d1]], axis=0)
-            o = jnp.dot(mats[k, pair], x, preferred_element_type=F32)
+            o = jnp.dot(mats[k, begin // 2 + i], x, preferred_element_type=F32)
             for d, part in ((d0, o[0:64]), (d1, o[64:128])):
                 total = combine(part)
                 if k == sections - 1:
@@ -623,6 +653,19 @@
                 else:
                     state[1 - now, d] = expand(total)
 
+    near, away = side * halves, (1 - side) * halves
+    for begin, small_which, count in ((near, 7, halves - 1), (away, 0, halves)):
+        finish(small.at[pl.ds(0, count), side_part], small_which, 1)
+        leaves(begin)
+        make_hot(lambda d: small[d, 3:4, :], lambda d: small[d, 4:5, :], begin, halves)
+    for begin, vals_which, count in ((near, 8, halves - 1), (away, 1, halves)):
+        arrived = pl.ds(0, count)
+        finish(vals.at[arrived], vals_which, 1)
+        gather(begin)
+        for k in range(sections - 1):
+            section(k, begin, halves)
+    next_reduce(rb_recv, rb_total, rb_joined, 9, 2)
+    section(sections - 1, 0, devices)
     tile_lane = lax.broadcasted_iota(jnp.int32, (half, 2 * LANES), 1)
     tile_masks = [jnp.where((tile_lane % LANES) // WIDTH == t, 1.0, 0.0).astype(BF16) for t in range(4)]
     zero = jnp.zeros((columns, LANES), F32)
@@ -648,28 +691,34 @@
             place_values(d, slice(LANES * d, LANES * (d + 1)), img)
             inner, square, energy = inner + v * img, square + v * v, energy + img * img
 
+    to_all(lambda d: image.at[d], back.at[me], 5, (3, 2, 1, 0))
     packed = zero
     for i, value in enumerate((inner, square, energy)):
         packed = jnp.where(lanes_q == rows_q + columns * i, jnp.sum(value, axis=1, keepdims=True), packed)
     sum_send[...] = jnp.sum(packed, axis=0, keepdims=True)
-    to_all(lambda d: sum_send, lambda d: sum_recv.at[d], 3)
-    sum_recv[me] = sum_send[...]
-
-    to_all(lambda d: image.at[d], lambda d: back.at[d], 5, (3,))
     image_sketch = sketch_product()
-    pieces_of(image_sketch, ri_send)
-    to_all(lambda d: ri_send.at[d], lambda d: ri_recv.at[d], 4)
-    ri_recv[me] = ri_send[me]
-    to_all(lambda d: image.at[d], lambda d: back.at[d], 5, (2, 1, 0))
+    start_reduce(image_sketch, ri_send, ri_recv, 4)
+    to_plane(lambda d: sum_send, sum_recv.at[seat], 3)
+    sum_recv[seat] = sum_send[...]
     back[me] = image[me]
 
-    finish(small_send.at[others, side_part], 0, 0)
-    finish(vals.at[others], 1, 0)
-    finish(rb_send.at[others], 2, 0)
-    finish(rb_recv.at[others], 2, 1)
-    finish(sum_recv.at[others], 3, 0)
-    finish(sum_recv.at[others], 3, 1)
-    totals = jnp.sum(sum_recv[...], axis=0)
+    finish(small_send.at[pl.ds(0, halves), side_part], 0, 0)
+    finish(small_send.at[pl.ds(0, halves - 1), side_part], 7, 0)
+    finish(vals.at[pl.ds(0, halves)], 1, 0)
+    finish(vals.at[pl.ds(0, halves - 1)], 8, 0)
+    finish(rb_send.at[mates], 2, 0)
+    next_reduce(ri_recv, ri_total, ri_joined, 11, 4)
+    finish(sum_recv.at[mates], 3, 1)
+    sum_total[...] = jnp.sum(sum_recv[...], axis=0)
+    to_planes(sum_total, sum_joined.at[plane], 10)
+    sum_joined[plane] = sum_total[...]
+    finish(rb_joined.at[peers], 9, 0)
+    finish(rb_joined.at[peers], 9, 1)
+    finish(sum_recv.at[mates], 3, 0)
+    finish(ri_send.at[mates], 4, 0)
+    basis_total = jnp.sum(rb_joined[...], axis=0)
+    finish(sum_joined.at[peers], 10, 1)
+    totals = jnp.sum(sum_joined[...], axis=0)
 
     def column(i):
         picked = jnp.where(lanes_q == rows_q + columns * i, jnp.broadcast_to(totals, (columns, LANES)), 0.0)
@@ -682,42 +731,34 @@
     inverse = 1.0 / spread
     for i, value in enumerate((projection, spread)):
         arn_ref[i:i + 1, :] = jnp.sum(jnp.where(lanes_q == rows_q, value, 0.0), axis=0, keepdims=True)[:, :columns]
-    proj[0] = projection
-    proj[1] = inverse * factor
-    mine = pl.ds(pl.multiple_of(lax.rem((me // part_tiles) * rows_each, columns), rows_each), rows_each)
-    base = jnp.sum(rb_recv[...], axis=0) * proj[0, mine, :]
-
-    finish(ri_recv.at[others], 4, 1)
-    own_chunk[...] = (jnp.sum(ri_recv[...], axis=0) - base) * proj[1, mine, :]
-    to_all(lambda d: own_chunk, lambda d: ag_recv.at[d], 6)
-    ag_recv[me] = own_chunk[...]
+    finish(ri_joined.at[peers], 11, 1)
+    wide = lambda x: jnp.concatenate([x] * (LOW // LANES), axis=1)
+    own_chunk[...] = (jnp.sum(ri_joined[...], axis=0) - basis_total * wide(projection)) * wide(factor * inverse)
+    to_plane(lambda d: own_chunk, ag_recv.at[seat], 6)
+    ag_recv[seat] = own_chunk[...]
     finish(back.at[others], 5, 1)
     for e in range(devices):
         here = slice(e * LANES, (e + 1) * LANES)
         nb_ref[:, here] = (back[e] - projection * v_ref[:, here]) * inverse
     finish(image.at[others], 5, 0)
-    finish(ri_send.at[others], 4, 0)
-    finish(ag_recv.at[others], 6, 0)
-    finish(ag_recv.at[others], 6, 1)
-    for n in range(devices):
-        flat = n * rows_each
-        tile, row = flat // 8, flat % 8
-        strip, side = tile // part_tiles, tile % part_tiles
-        top = strip * 8 + row
-        q0, high = top % columns, top // columns
-        begin = high * LOW + side * LANES
-        sketch_ref[q0:q0 + rows_each, begin:begin + LANES] = ag_recv[n]
+    finish(ri_joined.at[peers], 11, 0)
+    finish(sum_joined.at[peers], 10, 0)
+    finish(ag_recv.at[mates], 6, 0)
+    finish(ag_recv.at[mates], 6, 1)
+    for n in range(plane_size):
+        sketch_ref[:, LOW * n:LOW * (n + 1)] = ag_recv[n]
 
 
 def together(devices, basis_vector, diagonal, coords, phase_scale, sketch_rows, sketch_signs):
     columns, local_points = basis_vector.shape
     sections = devices.bit_length() - 1
     plane = (local_points // LANES, LANES)
-    rows_each = HIGH * columns * LOW // LANES // devices
     far = pl.BlockSpec(memory_space=pltpu.HBM)
     vmem = pl.BlockSpec(memory_space=pltpu.VMEM)
     tile = pltpu.VMEM((devices, columns, LANES), F32)
-    chunk = pltpu.VMEM((devices, rows_each, LANES), F32)
+    chunk = (columns, LOW)
+    pieces = pltpu.VMEM((HIGH,) + chunk, F32)
+    reduce_parts = [pieces, pieces, pltpu.VMEM(chunk, F32), pltpu.VMEM((devices // HIGH,) + chunk, F32)]
     return pl.pallas_call(
         functools.partial(tile_kernel, devices, local_points * devices),
         out_shape=(
@@ -745,12 +786,13 @@
             pltpu.VMEM((LOW, local_points), BF16),
             pltpu.VMEM((2 * HIGH * columns, local_points), BF16),
             pltpu.VMEM((devices, HIGH * columns, LANES), BF16),
-            pltpu.VMEM((2, columns, LANES), F32),
             pltpu.VMEM((1, LANES), F32),
-            pltpu.VMEM((devices, 1, LANES), F32),
-            chunk, chunk, chunk, chunk, chunk,
-            pltpu.VMEM((rows_each, LANES), F32),
-            pltpu.SemaphoreType.DMA((14,)),
+            pltpu.VMEM((HIGH, 1, LANES), F32),
+            pltpu.VMEM((1, LANES), F32),
+            pltpu.VMEM((devices // HIGH, 1, LANES), F32),
+            *reduce_parts, *reduce_parts, pieces,
+            pltpu.VMEM(chunk, F32),
+            pltpu.SemaphoreType.DMA((24,)),
             pltpu.SemaphoreType.DMA((5,)),
         ],
         compiler_params=pltpu.CompilerParams(

time: 39.5 us -> 37.3 us (0.944)
  Pallas kernels: 36.1 us -> 34 us
    pallas_call x1, Pallas kernels: 36.1 us -> 34 us  [together(): pl.pallas_call(functools.partial(tile_kernel, devices, local_points * dev...]
where the time goes in v3:
time: 37.3 us; the launch traced here: 37.2 us
  Pallas kernels  34 us (91%)
  local copies, waits for them, and re-layouts  1.92 us (5%)
  between operations  1.29 us (3%)
    pallas_call x1, Pallas kernels, together(): pl.pallas_call(functools.partial(tile_kernel, devices, local_points * dev...  34 us
    unnamed x3, local copies, waits for them, and re-layouts  1.92 us

profile of v3, /device:TPU:0, one launch (start us, length us, event | category | flops | bytes accessed | tf_op | source)
XLA Modules:
  0.0 37.2 jit_solution(9730967688847485932)
XLA Ops:
  1.3 34.0 %gmres.1 = (f32[16,4096]{1,0:T(8,128)S(1)}, f32[16,2048]{1,0:T(8,128)S(1)}, f32[2,16]{1,0:T(2,128)S(1)}) custom-call(s32[1]{0:T(128)S(6)} %copy.12.scale_ref, f32[16,4096]{1,0:T(8,128)} %v_in.1, s32[2,4096]{1,0:T(2,128)} %coords_in.1, f32[32,128]{1,0:T(8,128)} %bitcast.3, s32[32,128]{1,0:T(8,128)} %bitcast.4, s32[32,128]{1,0:T(8,128)} %bitcast.5), custom_call_target="tpu_custom_call" | custom-call | tf_op jit(solution)/shard_map/gmres/pallas_call | solution.py:762
  35.2 0.7 %copy.13 = f32[16,4096]{1,0:T(8,128)} copy(f32[16,4096]{1,0:T(8,128)S(1)} %get-tuple-element.6) | data formatting | bytes 524288
  36.0 0.7 %copy.14 = f32[16,2048]{1,0:T(8,128)} copy(f32[16,2048]{1,0:T(8,128)S(1)} %get-tuple-element.7) | data formatting | bytes 262144
  36.6 0.6 %copy.15 = f32[2,16]{1,0:T(2,128)} copy(f32[2,16]{1,0:T(2,128)S(1)} %get-tuple-element.8) | data formatting | bytes 256

commit v4 on v3

--- a/solution.py
+++ b/solution.py
@@ -451,7 +451,7 @@
 
     def to_all(source, target, which, aways):
         for away in aways:
-            there = facing(away)
+            there = {3: (1 - side) * (planes - 1), 2: 2 - side, 1: facing(1), 0: plane}[away]
 
             @pl.loop(0 if away else 1, plane_size)
             def _(i):
@@ -542,7 +542,7 @@
     pl.semaphore_wait(barrier, devices - 1)
     for which, aways in ((0, (3, 2)), (7, (1, 0))):
         to_all(lambda d: small_send.at[d, side_part], small.at[me, side_part], which, aways)
-    for which, aways in ((1, (3, 2)), (8, (1, 0))):
+    for which, aways in ((8, (1, 0)), (1, (3, 2))):
         to_all(lambda d: columns_at(v_ref, d), vals.at[me], which, aways)
     small[me] = small_send[me]
     vals[me] = columns_at(v_ref, me)[...]
@@ -554,19 +554,21 @@
     def place(tile):
         return pl.ds(pl.multiple_of(tile * LANES, LANES), LANES)
 
+    low_ids = lax.broadcasted_iota(jnp.int32, (LOW, LANES), 0).astype(F32).astype(BF16)
+    high_ids = (lax.broadcasted_iota(jnp.int32, (HIGH * columns, LANES), 0) // columns).astype(F32).astype(BF16)
+    one, nil = jnp.array(1.0, BF16), jnp.array(0.0, BF16)
+
     def make_hot(row_of, sign_of, begin, count):
-        @pl.loop(0, count)
+        @pl.loop(0, count, unroll=2)
         def _(i):
             d = begin + i
             row = row_of(d)
             high = jnp.floor(row * (1.0 / LOW))
-            low = (row - high * LOW).astype(jnp.int32)
-            ids = lax.broadcasted_iota(jnp.int32, (LOW, LANES), 0)
-            hot[:, place(d)] = jnp.where(ids == low, 1.0, 0.0).astype(BF16)
-            sign = jnp.broadcast_to(2.0 * sign_of(d) - 1.0, (columns, LANES))
-            wide = jnp.broadcast_to(high, (columns, LANES))
-            for g in range(HIGH):
-                masks[d, columns * g:columns * (g + 1), :] = jnp.where(wide == float(g), sign, 0.0).astype(BF16)
+            low = jnp.broadcast_to((row - high * LOW).astype(BF16), (LOW, LANES))
+            hot[:, place(d)] = jnp.where(low_ids == low, one, nil)
+            sign = jnp.broadcast_to((2.0 * sign_of(d) - 1.0).astype(BF16), (HIGH * columns, LANES))
+            wide = jnp.broadcast_to(high.astype(BF16), (HIGH * columns, LANES))
+            masks[d] = jnp.where(high_ids == wide, sign, nil)
 
     def place_values(d, at, value):
         top, rest = split(value)
@@ -619,7 +621,7 @@
         return jnp.concatenate([y * m for m in column_masks], axis=0)
 
     def leaves(begin):
-        @pl.loop(0, halves)
+        @pl.loop(0, halves, unroll=4)
         def _(i):
             d = begin + i
             pair = fold(small[d, 0:2, :].astype(jnp.int32) * scale).astype(F32)
@@ -691,7 +693,7 @@
             place_values(d, slice(LANES * d, LANES * (d + 1)), img)
             inner, square, energy = inner + v * img, square + v * v, energy + img * img
 
-    to_all(lambda d: image.at[d], back.at[me], 5, (3, 2, 1, 0))
+    to_all(lambda d: image.at[d], back.at[me], 5, (3, 2))
     packed = zero
     for i, value in enumerate((inner, square, energy)):
         packed = jnp.where(lanes_q == rows_q + columns * i, jnp.sum(value, axis=1, keepdims=True), packed)
@@ -699,6 +701,7 @@
     image_sketch = sketch_product()
     start_reduce(image_sketch, ri_send, ri_recv, 4)
     to_plane(lambda d: sum_send, sum_recv.at[seat], 3)
+    to_all(lambda d: image.at[d], back.at[me], 5, (1, 0))
     sum_recv[seat] = sum_send[...]
     back[me] = image[me]
 
@@ -749,6 +752,14 @@
         sketch_ref[:, LOW * n:LOW * (n + 1)] = ag_recv[n]
 
 
+def deliver(*refs):
+    copies = [pltpu.make_async_copy(refs[i], refs[3 + i], refs[6].at[i]) for i in range(3)]
+    for copy in copies:
+        copy.start()
+    for copy in copies:
+        copy.wait()
+
+
 def together(devices, basis_vector, diagonal, coords, phase_scale, sketch_rows, sketch_signs):
     columns, local_points = basis_vector.shape
     sections = devices.bit_length() - 1
@@ -759,7 +770,7 @@
     chunk = (columns, LOW)
     pieces = pltpu.VMEM((HIGH,) + chunk, F32)
     reduce_parts = [pieces, pieces, pltpu.VMEM(chunk, F32), pltpu.VMEM((devices // HIGH,) + chunk, F32)]
-    return pl.pallas_call(
+    results = pl.pallas_call(
         functools.partial(tile_kernel, devices, local_points * devices),
         out_shape=(
             jax.ShapeDtypeStruct((columns, local_points), F32),
@@ -801,6 +812,15 @@
     )(phase_scale, *(pltpu.with_memory_space_constraint(x, pltpu.HBM) for x in (
         basis_vector, coords, diagonal.reshape(plane), sketch_rows.reshape(plane),
         sketch_signs.reshape(plane))))
+    return pl.pallas_call(
+        deliver,
+        out_shape=[jax.ShapeDtypeStruct(x.shape, x.dtype) for x in results],
+        in_specs=[vmem] * 3,
+        out_specs=[far] * 3,
+        scratch_shapes=[pltpu.SemaphoreType.DMA((3,))],
+        compiler_params=pltpu.CompilerParams(vmem_limit_bytes=2**20),
+        name="deliver",
+    )(*results)
 
 
 def body(basis_vector, diagonal, coords, phase_scale, sketch_rows, sketch_signs):

time: 37.3 us -> 35.8 us (0.960)
  local copies, waits for them, and re-layouts: 1.92 us -> 0 us
  Pallas kernels: 34 us -> 34.4 us
    unnamed x3 -> x0, local copies, waits for them, and re-layouts: 1.92 us -> none
    pallas_call x0 -> x1, Pallas kernels: none -> 0.77 us  [together(): pl.pallas_call(deliver, out_shape=[jax.ShapeDtypeStruct(x.shape, x.dtype)...]
where the time goes in v4:
time: 35.8 us; the launch traced here: 35.7 us
  Pallas kernels  34.4 us (96%)
  between operations  1.29 us (4%)
    pallas_call x1, Pallas kernels, together(): pl.pallas_call(functools.partial(tile_kernel, devices, local_points * dev...  33.6 us
    pallas_call x1, Pallas kernels, together(): pl.pallas_call(deliver, out_shape=[jax.ShapeDtypeStruct(x.shape, x.dtype)...  0.77 us

profile of v4, /device:TPU:0, one launch (start us, length us, event | category | flops | bytes accessed | tf_op | source)
XLA Modules:
  0.0 35.7 jit_solution(18209079443087273979)
XLA Ops:
  1.3 33.6 %gmres.1 = (f32[16,4096]{1,0:T(8,128)S(1)}, f32[16,2048]{1,0:T(8,128)S(1)}, f32[2,16]{1,0:T(2,128)S(1)}) custom-call(s32[1]{0:T(128)S(6)} %copy.9.scale_ref, f32[16,4096]{1,0:T(8,128)} %v_in.1, s32[2,4096]{1,0:T(2,128)} %coords_in.1, f32[32,128]{1,0:T(8,128)} %bitcast.3, s32[32,128]{1,0:T(8,128)} %bitcast.4, s32[32,128]{1,0:T(8,128)} %bitcast.5), custom_call_target="tpu_custom_call" | custom-call | tf_op jit(solution)/shard_map/gmres/pallas_call | solution.py:773
  34.9 0.8 %deliver.1 = (f32[16,4096]{1,0:T(8,128)}, f32[16,2048]{1,0:T(8,128)}, f32[2,16]{1,0:T(2,128)}) custom-call(f32[16,4096]{1,0:T(8,128)S(1)} %get-tuple-element.6.refs_0_, f32[16,2048]{1,0:T(8,128)S(1)} %get-tuple-element.7.refs_1_, f32[2,16]{1,0:T(2,128)S(1)} %get-tuple-element.8.refs_2_), custom_call_target="tpu_custom_call" | custom-call | tf_op jit(solution)/shard_map/deliver/pallas_call | solution.py:815

commit v5 on v4

--- a/solution.py
+++ b/solution.py
@@ -566,7 +566,8 @@
             high = jnp.floor(row * (1.0 / LOW))
             low = jnp.broadcast_to((row - high * LOW).astype(BF16), (LOW, LANES))
             hot[:, place(d)] = jnp.where(low_ids == low, one, nil)
-            sign = jnp.broadcast_to((2.0 * sign_of(d) - 1.0).astype(BF16), (HIGH * columns, LANES))
+            flip = (1 - 2 * (d // halves)).astype(F32)
+            sign = jnp.broadcast_to(((2.0 * sign_of(d) - 1.0) * flip).astype(BF16), (HIGH * columns, LANES))
             wide = jnp.broadcast_to(high.astype(BF16), (HIGH * columns, LANES))
             masks[d] = jnp.where(high_ids == wide, sign, nil)
 
@@ -578,8 +579,10 @@
             left[columns * (HIGH + g):columns * (HIGH + g + 1), at] = rest * mask
 
     def sketch_product():
-        o = lax.dot_general(left[...], hot[...], (((1,), (1,)), ((), ())), preferred_element_type=F32)
-        return o[:HIGH * columns] + o[HIGH * columns:]
+        points = left.shape[1] // 2
+        o = [lax.dot_general(left[:, part], hot[:, part], (((1,), (1,)), ((), ())), preferred_element_type=F32)
+             for part in (slice(0, points), slice(points, 2 * points))]
+        return (o[0][:HIGH * columns] + o[0][HIGH * columns:]) - (o[1][:HIGH * columns] + o[1][HIGH * columns:])
 
     factor = math.sqrt(SKETCH / total_points)
 
@@ -693,7 +696,7 @@
             place_values(d, slice(LANES * d, LANES * (d + 1)), img)
             inner, square, energy = inner + v * img, square + v * v, energy + img * img
 
-    to_all(lambda d: image.at[d], back.at[me], 5, (3, 2))
+    to_all(lambda d: image.at[d], back.at[me], 5, (3, 2, 1, 0))
     packed = zero
     for i, value in enumerate((inner, square, energy)):
         packed = jnp.where(lanes_q == rows_q + columns * i, jnp.sum(value, axis=1, keepdims=True), packed)
@@ -701,7 +704,6 @@
     image_sketch = sketch_product()
     start_reduce(image_sketch, ri_send, ri_recv, 4)
     to_plane(lambda d: sum_send, sum_recv.at[seat], 3)
-    to_all(lambda d: image.at[d], back.at[me], 5, (1, 0))
     sum_recv[seat] = sum_send[...]
     back[me] = image[me]
 

time: 35.8 us -> 35.3 us (0.986)
  Pallas kernels: 34.4 us -> 33.9 us
    pallas_call x1, Pallas kernels: 33.6 us -> 33.1 us  [together(): pl.pallas_call(functools.partial(tile_kernel, devices, local_points * dev...]
where the time goes in v5:
time: 35.3 us; the launch traced here: 35.2 us
  Pallas kernels  33.9 us (96%)
  between operations  1.29 us (4%)
    pallas_call x1, Pallas kernels, together(): pl.pallas_call(functools.partial(tile_kernel, devices, local_points * dev...  33.1 us
    pallas_call x1, Pallas kernels, together(): pl.pallas_call(deliver, out_shape=[jax.ShapeDtypeStruct(x.shape, x.dtype)...  0.77 us

profile of v5, /device:TPU:0, one launch (start us, length us, event | category | flops | bytes accessed | tf_op | source)
XLA Modules:
  0.0 35.2 jit_solution(14922606123488002063)
XLA Ops:
  1.3 33.1 %gmres.1 = (f32[16,4096]{1,0:T(8,128)S(1)}, f32[16,2048]{1,0:T(8,128)S(1)}, f32[2,16]{1,0:T(2,128)S(1)}) custom-call(s32[1]{0:T(128)S(6)} %copy.9.scale_ref, f32[16,4096]{1,0:T(8,128)} %v_in.1, s32[2,4096]{1,0:T(2,128)} %coords_in.1, f32[32,128]{1,0:T(8,128)} %bitcast.3, s32[32,128]{1,0:T(8,128)} %bitcast.4, s32[32,128]{1,0:T(8,128)} %bitcast.5), custom_call_target="tpu_custom_call" | custom-call | tf_op jit(solution)/shard_map/gmres/pallas_call | solution.py:775
  34.4 0.8 %deliver.1 = (f32[16,4096]{1,0:T(8,128)}, f32[16,2048]{1,0:T(8,128)}, f32[2,16]{1,0:T(2,128)}) custom-call(f32[16,4096]{1,0:T(8,128)S(1)} %get-tuple-element.6.refs_0_, f32[16,2048]{1,0:T(8,128)S(1)} %get-tuple-element.7.refs_1_, f32[2,16]{1,0:T(2,128)S(1)} %get-tuple-element.8.refs_2_), custom_call_target="tpu_custom_call" | custom-call | tf_op jit(solution)/shard_map/deliver/pallas_call | solution.py:817

commit v6 on v5

--- a/solution.py
+++ b/solution.py
@@ -453,13 +453,13 @@
         for away in aways:
             there = {3: (1 - side) * (planes - 1), 2: 2 - side, 1: facing(1), 0: plane}[away]
 
-            @pl.loop(0 if away else 1, plane_size)
+            @pl.loop(0 if away else 1, plane_size, unroll=True)
             def _(i):
                 other = plane_size * there + lax.rem(seat + i, plane_size)
                 send(source(other), target, which, other)
 
     def to_plane(source, target, which):
-        @pl.loop(1, plane_size)
+        @pl.loop(1, plane_size, unroll=True)
         def _(i):
             other = lax.rem(seat + i, plane_size)
             send(source(other), target, which, plane_size * plane + other)

time: 35.3 us -> 35.4 us (level)
  no operation moved by 1% of the time
where the time goes in v6:
time: 35.4 us; the launch traced here: 35.2 us
  Pallas kernels  33.9 us (96%)
  between operations  1.29 us (4%)
    pallas_call x1, Pallas kernels, together(): pl.pallas_call(functools.partial(tile_kernel, devices, local_points * dev...  33.1 us
    pallas_call x1, Pallas kernels, together(): pl.pallas_call(deliver, out_shape=[jax.ShapeDtypeStruct(x.shape, x.dtype)...  0.77 us

profile of v6, /device:TPU:0, one launch (start us, length us, event | category | flops | bytes accessed | tf_op | source)
XLA Modules:
  0.0 35.2 jit_solution(7581876381118658510)
XLA Ops:
  1.3 33.1 %gmres.1 = (f32[16,4096]{1,0:T(8,128)S(1)}, f32[16,2048]{1,0:T(8,128)S(1)}, f32[2,16]{1,0:T(2,128)S(1)}) custom-call(s32[1]{0:T(128)S(6)} %copy.9.scale_ref, f32[16,4096]{1,0:T(8,128)} %v_in.1, s32[2,4096]{1,0:T(2,128)} %coords_in.1, f32[32,128]{1,0:T(8,128)} %bitcast.3, s32[32,128]{1,0:T(8,128)} %bitcast.4, s32[32,128]{1,0:T(8,128)} %bitcast.5), custom_call_target="tpu_custom_call" | custom-call | tf_op jit(solution)/shard_map/gmres/pallas_call | solution.py:775
  34.4 0.8 %deliver.1 = (f32[16,4096]{1,0:T(8,128)}, f32[16,2048]{1,0:T(8,128)}, f32[2,16]{1,0:T(2,128)}) custom-call(f32[16,4096]{1,0:T(8,128)S(1)} %get-tuple-element.6.refs_0_, f32[16,2048]{1,0:T(8,128)S(1)} %get-tuple-element.7.refs_1_, f32[2,16]{1,0:T(2,128)S(1)} %get-tuple-element.8.refs_2_), custom_call_target="tpu_custom_call" | custom-call | tf_op jit(solution)/shard_map/deliver/pallas_call | solution.py:817

commit v7 on v5

--- a/solution.py
+++ b/solution.py
@@ -696,7 +696,7 @@
             place_values(d, slice(LANES * d, LANES * (d + 1)), img)
             inner, square, energy = inner + v * img, square + v * v, energy + img * img
 
-    to_all(lambda d: image.at[d], back.at[me], 5, (3, 2, 1, 0))
+    to_all(lambda d: image.at[d], back.at[me], 5, (3, 2))
     packed = zero
     for i, value in enumerate((inner, square, energy)):
         packed = jnp.where(lanes_q == rows_q + columns * i, jnp.sum(value, axis=1, keepdims=True), packed)
@@ -713,6 +713,7 @@
     finish(vals.at[pl.ds(0, halves - 1)], 8, 0)
     finish(rb_send.at[mates], 2, 0)
     next_reduce(ri_recv, ri_total, ri_joined, 11, 4)
+    to_all(lambda d: image.at[d], back.at[me], 5, (1, 0))
     finish(sum_recv.at[mates], 3, 1)
     sum_total[...] = jnp.sum(sum_recv[...], axis=0)
     to_planes(sum_total, sum_joined.at[plane], 10)

time: 35.3 us -> 35.3 us (level)
  no operation moved by 1% of the time
where the time goes in v7:
time: 35.3 us; the launch traced here: 35.2 us
  Pallas kernels  33.9 us (96%)
  between operations  1.29 us (4%)
    pallas_call x1, Pallas kernels, together(): pl.pallas_call(functools.partial(tile_kernel, devices, local_points * dev...  33.1 us
    pallas_call x1, Pallas kernels, together(): pl.pallas_call(deliver, out_shape=[jax.ShapeDtypeStruct(x.shape, x.dtype)...  0.77 us

profile of v7, /device:TPU:0, one launch (start us, length us, event | category | flops | bytes accessed | tf_op | source)
XLA Modules:
  0.0 35.2 jit_solution(15376387219311236544)
XLA Ops:
  1.3 33.1 %gmres.1 = (f32[16,4096]{1,0:T(8,128)S(1)}, f32[16,2048]{1,0:T(8,128)S(1)}, f32[2,16]{1,0:T(2,128)S(1)}) custom-call(s32[1]{0:T(128)S(6)} %copy.9.scale_ref, f32[16,4096]{1,0:T(8,128)} %v_in.1, s32[2,4096]{1,0:T(2,128)} %coords_in.1, f32[32,128]{1,0:T(8,128)} %bitcast.3, s32[32,128]{1,0:T(8,128)} %bitcast.4, s32[32,128]{1,0:T(8,128)} %bitcast.5), custom_call_target="tpu_custom_call" | custom-call | tf_op jit(solution)/shard_map/gmres/pallas_call | solution.py:776
  34.4 0.8 %deliver.1 = (f32[16,4096]{1,0:T(8,128)}, f32[16,2048]{1,0:T(8,128)}, f32[2,16]{1,0:T(2,128)}) custom-call(f32[16,4096]{1,0:T(8,128)S(1)} %get-tuple-element.6.refs_0_, f32[16,2048]{1,0:T(8,128)S(1)} %get-tuple-element.7.refs_1_, f32[2,16]{1,0:T(2,128)S(1)} %get-tuple-element.8.refs_2_), custom_call_target="tpu_custom_call" | custom-call | tf_op jit(solution)/shard_map/deliver/pallas_call | solution.py:818
